TPU v7x, 256 devices: a whole 4x4x8 slice. The times are simulated.
256 devices in a mesh: shot: 32 (over y, z), depth: 8 (over x, core).
Axes of the slice: x: 4, y: 4, z: 8, core: 2. Of those that a mesh axis runs over, the one named last changes fastest.
Arguments:
- correlation: float32 [64, 64, 32, 1024], P('shot', None, None, 'depth'), may hold values from -6 to 6
- illumination: float32 [64, 64, 32, 1024], P('shot', None, None, 'depth'), may hold values from 0.25 to 4
- aperture: int32 [64, 4], P('shot'), may hold values from 0 to 64, as said below
Outputs:
- stack: float32 [64, 32, 1024], P('shot', None, 'depth')
Inputs may be any that keep to these rules, and one draw needn't show every extreme that they name: For every shot, 0 <= aperture[s,0] < aperture[s,1] <= 64 and 0 <= aperture[s,2] < aperture[s,3] <= 32; each box spans a quarter to a half of the grid along each of the two dimensions.
All inputs are finite; a program needn't handle non-finite values.
Results may differ from a plain program's by a relative error of at most 0.0003.
Values sent between devices are 32-bit elements.
A program may use at most 64 MiB of HBM per device.

v0:
```python
import math

import jax
import jax.numpy as jnp
from jax import lax
from jax.sharding import PartitionSpec as P


def padded_2(block, sides, width):
    for axis, dim in sides:
        count = lax.axis_size(axis)
        forward = [(i, i + 1) for i in range(count - 1)]
        backward = [(target, source) for source, target in forward]
        low = lax.ppermute(
            lax.slice_in_dim(block, block.shape[dim] - width, None, axis=dim), axis, forward
        )
        high = lax.ppermute(lax.slice_in_dim(block, 0, width, axis=dim), axis, backward)
        block = jnp.concatenate([low, block, high], axis=dim)
    return block


def sent_to_all(array, axis):
    copies = jnp.broadcast_to(array, (lax.axis_size(axis), *array.shape))
    return lax.all_to_all(copies, axis, split_axis=0, concat_axis=0, tiled=True)


def of_everyone(array, axis):
    everything = sent_to_all(array, axis)
    return jnp.sum(everything, axis=0)


def taken_together(array, axis):
    return sent_to_all(array, axis).max(axis=0)


def in_blocks(array, dim, devices):
    before, after = (array.shape[:dim], array.shape[dim + 1 :])
    return jnp.moveaxis(array.reshape(*before, devices, -1, *after), dim, 0)


def summed_on_arrival(array, axis, dim):
    devices = lax.axis_size(axis)
    blocks = lax.all_to_all(in_blocks(array, dim, devices), axis, 0, 0, tiled=True)
    return jnp.sum(blocks, axis=0)


def on_device(correlation, illumination, aperture):
    shots, rows, cols, slab = correlation.shape
    first = lax.broadcasted_iota(jnp.int32, (1, rows, cols, 1), 1)
    second = lax.broadcasted_iota(jnp.int32, (1, rows, cols, 1), 2)
    bounds = aperture.reshape(shots, 4, 1, 1, 1)
    inside = (
        (first >= bounds[:, 0])
        & (first < bounds[:, 1])
        & (second >= bounds[:, 2])
        & (second < bounds[:, 3])
    )
    normalized = inside.astype(jnp.float32) * correlation / (illumination + 0.1)
    padded = padded_2(normalized, (("depth", 3),), 1)
    padded = jnp.pad(padded, ((0, 0), (1, 1), (1, 1), (0, 0)))
    beside = padded[:, 2:, 1:-1, 1:-1] + padded[:, :-2, 1:-1, 1:-1]
    beside = beside + padded[:, 1:-1, 2:, 1:-1] + padded[:, 1:-1, :-2, 1:-1]
    beside = beside + padded[:, 1:-1, 1:-1, 2:] + padded[:, 1:-1, 1:-1, :-2]
    filtered = 6.0 * normalized - beside
    local_energy = jnp.sum(filtered * filtered, axis=(1, 2, 3))
    cells = rows * cols * slab * lax.axis_size("depth")
    total_shots = shots * lax.axis_size("shot")
    meansq = of_everyone(local_energy, "depth") / cells
    peak = taken_together(jnp.max(meansq), "shot")
    weight = 1.0 / jnp.sqrt(meansq + 0.5 * peak + 1.0)
    weighted = jnp.sum(weight.reshape(shots, 1, 1, 1) * filtered, axis=0) / math.sqrt(total_shots)
    return summed_on_arrival(weighted, "shot", 0)


def solution(mesh):
    return jax.shard_map(
        on_device,
        mesh=mesh,
        in_specs=(P("shot", None, None, "depth"), P("shot", None, None, "depth"), P("shot", None)),
        out_specs=P("shot", None, "depth"),
        check_vma=False,
    )
```

profile of v0, /device:TPU:4, one launch (start us, length us, event | category | flops | bytes accessed | tf_op | source)
XLA Modules:
  0.0 97.5 jit_solution(1868968791001005446)
XLA Ops:
  0.0 0.0 copy-start
  0.0 1.1 %slice_reduce_fusion.3 = (s32[2]{0:T(128)S(1)}, s32[2]{0:T(128)S(1)}, s32[2]{0:T(128)S(1)}, s32[2]{0:T(128)S(1)}) fusion(s32[2,4,1,1,1]{1,0,4,3,2:T(2,128)} %bitcast.3), kind=kLoop, calls=%fused_computation.32 | loop fusion | bytes 64 | tf_op jit(solution)/shard_map/slice | solution.py:53
  1.1 5.6 %copy.19 = f32[2,64,32,128]{1,2,3,0:T(8,128)} copy(f32[2,64,32,128]{3,2,1,0:T(8,128)} %param.3) | data formatting | bytes 4194304 | tf_op args[0]
  6.7 0.0 copy-done
  6.7 4.5 %copy.20 = f32[2,64,32,128]{1,2,3,0:T(8,128)} copy(f32[2,64,32,128]{3,2,1,0:T(8,128)S(1)} %copy-done) | data formatting | bytes 4194304 | tf_op args[1]
  11.2 0.1 fusion.9
  11.2 4.5 %add_divide_fusion = f32[2,64,32,128]{1,2,3,0:T(8,128)S(1)} fusion(f32[2,64,32,128]{1,2,3,0:T(8,128)} %copy.20, f32[2,64,32,128]{1,2,3,0:T(8,128)} %copy.19, f32[2,64,32]{1,2,0:T(8,128)S(1)} %fusion.9), kind=kLoop, calls=%fused_computation.19 | loop fusion | flops 1572864 | bytes 6307840 | tf_op jit(solution)/shard_map/div | solution.py:58
  15.8 1.9 %collective-permute-start.1 = (f32[2,64,32,1]{1,2,3,0:T(8,128)S(1)}, f32[2,64,32,1]{1,2,3,0:T(8,128)S(1)}, u32[]{:S(2)}, u32[]{:S(2)}) collective-permute-start(f32[2,64,32,1]{1,2,3,0:T(8,128)S(1)} %get-tuple-element.11), channel_id=1, source_target_pairs={{1,0},{2,1},{3,2},{4,3},{5,4},{6,5},{7,6},{9,8},{10,9},{11,10},{12... | collective-permute-start | bytes 49160 | tf_op jit(solution)/shard_map/ppermute | solution.py:17
  17.7 2.4 %collective-permute-start = (f32[2,64,32,1]{1,2,3,0:T(8,128)S(1)}, f32[2,64,32,1]{1,2,3,0:T(8,128)S(1)}, u32[]{:S(2)}, u32[]{:S(2)}) collective-permute-start(f32[2,64,32,1]{1,2,3,0:T(8,128)S(1)} %get-tuple-element.12), channel_id=1, source_target_pairs={{0,1},{1,2},{2,3},{3,4},{4,5},{5,6},{6,7},{8,9},{9,10},{10,11},{11... | collective-permute-start | bytes 49160 | tf_op jit(solution)/shard_map/ppermute | solution.py:14
  20.1 0.0 collective-permute-done.1
  20.1 2.8 %collective-permute-done = f32[2,64,32,1]{1,2,3,0:T(8,128)S(1)} collective-permute-done((f32[2,64,32,1]{1,2,3,0:T(8,128)S(1)}, f32[2,64,32,1]{1,2,3,0:T(8,128)S(1)}, u32[]{:S(2)}, u32[]{:S(2)}) %collective-permute-start) | collective-permute-done | bytes 16416 | tf_op jit(solution)/shard_map/ppermute | solution.py:14
  23.0 2.2 %select_maximum_fusion = f32[2,66,34,130]{1,2,3,0:T(8,128)S(1)} fusion(f32[2,64,32,1]{1,2,3,0:T(8,128)S(1)} %collective-permute-done.1, f32[2,64,32,128]{1,2,3,0:T(8,128)S(1)} %add_divide_fusion, f32[2,64,32,1]{1,2,3,0:T(8,128)S(1)} %collective-permute-done), kind=kLoop, calls=%fused_computation.4 | loop fusion | flops 8751600 | bytes 4463680 | tf_op jit(solution)/shard_map/concatenate | solution.py:18
  25.2 5.1 %multiply_reduce_fusion.1 = (f32[2]{0:T(128)S(1)}, f32[2,64,32,128]{1,2,3,0:T(8,128)}) fusion(f32[2,64,32,128]{1,2,3,0:T(8,128)S(1)} %add_divide_fusion, f32[2,64,32,1]{1,2,3,0:T(8,128)S(1)} %collective-permute-done, f32[2,64,32,1]{1,2,3,0:T(8,128)S(1)} %collective-permute-done.1, f32[2,66,34,130]{1,2,3,0:T(8,128)S(1)} %select_maximum_fusion), kind=kLoop, calls=%fused_computation.18 | loop fusion | flops 5767166 | bytes 12615688 | tf_op jit(solution)/shard_map/reduce_sum | solution.py:65
  30.3 7.5 %all_to_all.17 = f32[8,1,2]{2,1,0:T(1,128)S(1)} all-to-all(f32[8,1,2]{2,1,0:T(1,128)S(1)} %broadcast_in_dim.6), channel_id=1, replica_groups=mesh['shot'=32,'depth'=8] {'depth'}, dimensions={0} | all-to-all | bytes 128 | tf_op jit(solution)/shard_map/all_to_all | solution.py:24
  37.8 0.6 multiply_reduce_fusion.2
  38.4 0.7 broadcast_in_dim.7
  39.1 21.1 %all_to_all.18 = f32[32,1,1]{2,1,0:T(1,128)S(1)} all-to-all(f32[32,1,1]{2,1,0:T(1,128)S(1)} %broadcast_in_dim.7), channel_id=1, replica_groups=mesh['shot'=32,'depth'=8] {'shot'}, dimensions={0} | all-to-all | bytes 256 | tf_op jit(solution)/shard_map/all_to_all | solution.py:24
  60.2 0.6 reduce_max.19
  61.5 3.1 %multiply_reduce_fusion = f32[64,32,128]{0,1,2:T(8,128)S(1)} fusion(f32[2,64,32,128]{1,2,3,0:T(8,128)} %get-tuple-element.10, f32[2]{0:T(128)S(1)} %add_rsqrt_fusion), kind=kLoop, calls=%fused_computation.17 | loop fusion | flops 786432 | bytes 3145736 | tf_op jit(solution)/shard_map/reduce_sum | solution.py:71
  64.6 1.6 %copy.23 = f32[64,32,128]{2,1,0:T(8,128)S(1)} copy(f32[64,32,128]{0,1,2:T(8,128)S(1)} %multiply_reduce_fusion) | data formatting | bytes 2097152 | tf_op jit(solution)/shard_map/reduce_sum | solution.py:71
  66.2 0.1 broadcast_multiply_fusion
  66.3 30.5 %all_to_all.19 = f32[32,2,32,128]{3,2,1,0:T(8,128)S(1)} all-to-all(f32[32,2,32,128]{3,2,1,0:T(8,128)S(1)} %bitcast.2), channel_id=1, replica_groups=mesh['shot'=32,'depth'=8] {'shot'}, dimensions={0} | all-to-all | bytes 2097152 | tf_op jit(solution)/shard_map/all_to_all | solution.py:43
  96.8 0.7 reduce_sum.39
  (4 shorter events, 0.0 us)
Async XLA Ops:
  0.0 6.7 %copy-start = (f32[2,64,32,128]{3,2,1,0:T(8,128)S(1)}, f32[2,64,32,128]{3,2,1,0:T(8,128)}, u32[]{:S(2)}) copy-start(f32[2,64,32,128]{3,2,1,0:T(8,128)} %param.4) | copy-start | bytes 6291460
  15.8 4.3 %collective-permute-start.1 = (f32[2,64,32,1]{1,2,3,0:T(8,128)S(1)}, f32[2,64,32,1]{1,2,3,0:T(8,128)S(1)}, u32[]{:S(2)}, u32[]{:S(2)}) collective-permute-start(f32[2,64,32,1]{1,2,3,0:T(8,128)S(1)} %get-tuple-element.11), channel_id=1, source_target_pairs={{1,0},{2,1},{3,2},{4,3},{5,4},{6,5},{7,6},{9,8},{10,9},{11,10},{12... | collective-permute-start | bytes 49160 | tf_op jit(solution)/shard_map/ppermute | solution.py:17
  17.7 5.2 %collective-permute-start = (f32[2,64,32,1]{1,2,3,0:T(8,128)S(1)}, f32[2,64,32,1]{1,2,3,0:T(8,128)S(1)}, u32[]{:S(2)}, u32[]{:S(2)}) collective-permute-start(f32[2,64,32,1]{1,2,3,0:T(8,128)S(1)} %get-tuple-element.12), channel_id=1, source_target_pairs={{0,1},{1,2},{2,3},{3,4},{4,5},{5,6},{6,7},{8,9},{9,10},{10,11},{11... | collective-permute-start | bytes 49160 | tf_op jit(solution)/shard_map/ppermute | solution.py:14
where the time goes:
time: 99.5 us; the launch traced here: 97.5 us
  blocking collectives  59.1 us (59%)
  other arithmetic  17.1 us (17%)
  local copies, waits for them, and re-layouts  13.4 us (13%)
  starting transfers between devices  4.33 us (4%)
  waiting for transfers between devices  2.81 us (3%)
    all_to_all x1, blocking collectives, summed_on_arrival(): lax.all_to_all(in_blocks(array, dim, devices), axis, 0, 0, tiled=True)  30.5 us
    all_to_all x2, blocking collectives, sent_to_all(): return lax.all_to_all(copies, axis, split_axis=0, concat_axis=0, tiled=True)  28.6 us
    unnamed x4, local copies, waits for them, and re-layouts  10.1 us
    reduce_sum x1, other arithmetic, on_device(): local_energy = jnp.sum(filtered * filtered, axis=(1, 2, 3))  5.09 us
    div x1, other arithmetic, on_device(): normalized = inside.astype(jnp.float32) * correlation / (illumination + 0.1)  4.53 us
    reduce_sum x1, other arithmetic, on_device(): jnp.sum(weight.reshape(shots, 1, 1, 1) * filtered, axis=0)  3.08 us
    ppermute x1, waiting for transfers between devices, padded_2(): lax.ppermute(lax.slice_in_dim(block, block.shape[dim] - width, None, axis...  2.81 us
    ppermute x1, starting transfers between devices, padded_2(): lax.ppermute(lax.slice_in_dim(block, block.shape[dim] - width, None, axis...  2.41 us
  transfers between devices with their start and end apart: 2, of which 1 were waited for; matrix products, arithmetic and copies ran while one was open for 0% of the time, Pallas kernels for 0%

commit v1 on v0

v1 whole, which is shorter than its diff:
```python
import functools

import jax
import jax.numpy as jnp
from jax import lax
from jax.experimental import pallas as pl
from jax.experimental.pallas import tpu as pltpu
from jax.sharding import PartitionSpec as P

ROWS_Y = 4
PIECES = 4
F32 = jnp.float32


def kernel(
    ny_dev, nz_dev, nd_dev,
    box, corr, illum, out,
    corr_v, illum_v, filt, edge, edge_low, edge_high, energy, peaks,
    raw_up, raw_down, weighted, got_up, got_down, image, arrived,
    load_sem, edge_send, edge_recv, small_send, small_recv,
    raw_send, raw_recv, move_send, move_recv, last_send, last_recv,
):
    shots, nx, ny, nz = filt.shape
    shot, depth = lax.axis_index("shot"), lax.axis_index("depth")
    y, z = shot // nz_dev, shot % nz_dev
    per_y = nx // ny_dev
    per_z = per_y // nz_dev
    half = per_y // 2

    step = nx // PIECES
    loads = []
    for s in range(shots):
        for c in range(PIECES):
            rows = pl.ds(c * step, step)
            pair = [
                pltpu.make_async_copy(corr.at[s, rows], corr_v.at[s, rows], load_sem.at[s, c, 0]),
                pltpu.make_async_copy(illum.at[s, rows], illum_v.at[s, rows], load_sem.at[s, c, 1]),
            ]
            for copy in pair:
                copy.start()
            loads.append(pair)

    near = []
    for dy in range(ny_dev):
        for dd in range(nd_dev):
            if dy or dd:
                near.append({
                    "shot": lax.rem(y + dy, ny_dev) * nz_dev + z,
                    "depth": lax.rem(depth + dd, nd_dev),
                })
    along = [
        {"shot": y * nz_dev + lax.rem(z + dz, nz_dev), "depth": depth} for dz in range(1, nz_dev)
    ]
    barrier = pltpu.get_barrier_semaphore()
    for peer in near + along:
        pl.semaphore_signal(barrier, inc=1, device_id=peer, device_id_type=pl.DeviceIdType.MESH)

    lane = lax.broadcasted_iota(jnp.int32, (ny, nz), 1)
    row = lax.broadcasted_iota(jnp.int32, (ny, nz), 0)
    first, last = lane == 0, lane == nz - 1
    top, bottom = row == 0, row == ny - 1
    column = lane // 2
    zero = jnp.zeros((ny, nz), F32)

    sums, packs = [], []
    for s in range(shots):
        low, high = box[s, 0], box[s, 1]
        strip = ((row >= box[s, 2]) & (row < box[s, 3])).astype(F32)

        def normal(x, s=s, low=low, high=high, strip=strip):
            inside = jnp.where((x >= low) & (x < high), 1.0, 0.0).astype(F32)
            return (strip * inside) * corr_v[s, x] / (illum_v[s, x] + 0.1)

        def filtered(before, here, after):
            beside = before + after
            beside = beside + jnp.where(top, 0.0, pltpu.roll(here, 1, 0))
            beside = beside + jnp.where(bottom, 0.0, pltpu.roll(here, ny - 1, 0))
            beside = beside + jnp.where(first, 0.0, pltpu.roll(here, 1, 1))
            beside = beside + jnp.where(last, 0.0, pltpu.roll(here, nz - 1, 1))
            return 6.0 * here - beside

        def one(x, after, carry, s=s):
            before, here, mine, rim, total = carry
            value = filtered(before, here, after)
            filt[s, x] = value
            chosen = column == x
            mine = jnp.where(chosen, pltpu.roll(here, lax.rem(2 * x + 1, nz), 1), mine)
            rim = jnp.where(chosen, pltpu.roll(value, lax.rem(2 * x + 1, nz), 1), rim)
            total = total + jnp.where(first | last, 0.0, value * value)
            return here, after, mine, rim, total

        for copy in loads[s * PIECES]:
            copy.wait()
        carry = (zero, normal(0), zero, zero, zero)
        for c in range(PIECES):
            if c:
                for copy in loads[s * PIECES + c]:
                    copy.wait()
            carry = lax.fori_loop(
                c * step + (c == 0), (c + 1) * step,
                lambda x, carry: one(x - 1, normal(x), carry), carry,
            )
        carry = one(nx - 1, zero, carry)
        edge[s] = carry[2]
        packs.append(carry[3])
        sums.append(carry[4])

    pl.semaphore_wait(barrier, len(near) + len(along))

    def remote(src, dst, send, recv, peer):
        return pltpu.make_async_remote_copy(
            src_ref=src, dst_ref=dst, send_sem=send, recv_sem=recv,
            device_id=peer, device_id_type=pl.DeviceIdType.MESH,
        )

    up = remote(edge, edge_low, edge_send.at[0], edge_recv.at[0], {"shot": shot, "depth": lax.rem(depth + 1, nd_dev)})
    down = remote(edge, edge_high, edge_send.at[1], edge_recv.at[1], {"shot": shot, "depth": lax.rem(depth + nd_dev - 1, nd_dev)})

    @pl.when(depth < nd_dev - 1)
    def _():
        up.start()

    @pl.when(depth > 0)
    def _():
        down.start()

    @pl.when(depth == 0)
    def _():
        edge_low[...] = jnp.zeros_like(edge_low)

    @pl.when(depth == nd_dev - 1)
    def _():
        edge_high[...] = jnp.zeros_like(edge_high)

    @pl.when(depth > 0)
    def _():
        up.wait_recv()

    @pl.when(depth < nd_dev - 1)
    def _():
        down.wait_recv()

    even = lax.rem(lane, 2) == 0
    sides = []
    for s in range(shots):
        side = jnp.where(even, pltpu.roll(edge_high[s], nz - 1, 1), pltpu.roll(edge_low[s], 1, 1))
        sides.append(side)
        rim = packs[s] - side
        energy[0, s : s + 1] = jnp.sum(sums[s] + rim * rim, axis=0, keepdims=True)

    spread = []
    for i, peer in enumerate(near):
        dy, dd = (i + 1) // nd_dev, (i + 1) % nd_dev
        slot = ((ny_dev - dy) % ny_dev) * nd_dev + (nd_dev - dd) % nd_dev
        copy = remote(energy.at[0], energy.at[slot], small_send.at[0], small_recv.at[0], peer)
        copy.start()
        spread.append(copy)

    ends = first | last

    def finish(base, count):
        def body(i, carry):
            x = base + i
            for s in range(shots):
                filt[s, x] = filt[s, x] - jnp.where(ends, pltpu.roll(sides[s], lax.rem(nz + nz - 1 - 2 * x, nz), 1), 0.0)
            return carry
        lax.fori_loop(0, count, body, 0)

    after = lax.rem(y + 1, ny_dev)
    before = lax.rem(y + ny_dev - 1, ny_dev)
    across = lax.rem(y + ny_dev // 2, ny_dev)
    next_y = {"shot": after * nz_dev + z, "depth": depth}
    prev_y = {"shot": before * nz_dev + z, "depth": depth}
    finish(across * per_y, half)
    raw_a = remote(filt.at[:, pl.ds(across * per_y, half)], raw_up, raw_send.at[0], raw_recv.at[0], next_y)
    raw_a.start()
    finish(across * per_y + half, half)
    raw_b = remote(filt.at[:, pl.ds(across * per_y + half, half)], raw_down, raw_send.at[1], raw_recv.at[1], prev_y)
    raw_b.start()
    finish(after * per_y, per_y)
    finish(before * per_y, per_y)
    finish(y * per_y, per_y)

    others = energy.at[pl.ds(1, len(near))]
    pltpu.make_async_copy(others, others, small_recv.at[0]).wait()
    cells = nx * ny * nz * nd_dev
    means = []
    for dy in range(ny_dev):
        both = jnp.sum(energy[dy * nd_dev : (dy + 1) * nd_dev], axis=0)
        means.append(jnp.broadcast_to(jnp.sum(both, axis=1, keepdims=True) / cells, (shots, nz)))
    peak = functools.reduce(jnp.maximum, means)
    peaks[0] = peak
    for i, peer in enumerate(along):
        slot = nz_dev - 1 - i
        copy = remote(peaks.at[0], peaks.at[slot], small_send.at[1], small_recv.at[1], peer)
        copy.start()
    rest = peaks.at[pl.ds(1, len(along))]
    pltpu.make_async_copy(rest, rest, small_recv.at[1]).wait()
    peak = jnp.max(jnp.max(peaks[...], axis=0), axis=0, keepdims=True)
    scale = 1.0 / float(shots * ny_dev * nz_dev) ** 0.5
    weights = [scale / jnp.sqrt(mean + 0.5 * peak + 1.0) for mean in means]

    def weight(dy, s):
        return jnp.broadcast_to(weights[dy][s : s + 1], (ny, nz))

    def own(base, count, extra=None):
        mine = [weight(0, s) for s in range(shots)]

        def body(i, carry):
            x = base + i
            value = sum(mine[s] * filt[s, x] for s in range(shots))
            if extra is not None:
                ref, dy = extra
                value = value + sum(weight(dy, s) * ref[s, i] for s in range(shots))
            weighted[x] = value
            return carry
        lax.fori_loop(0, count, body, 0)

    def move(base, dst, sem, peer):
        copy = remote(weighted.at[pl.ds(base, half)], dst, move_send.at[sem], move_recv.at[sem], peer)
        copy.start()
        return copy

    moves = []
    own(after * per_y + half, half)
    moves.append(move(after * per_y + half, got_up.at[pl.ds(half, half)], 0, next_y))
    own(before * per_y, half)
    moves.append(move(before * per_y, got_down.at[pl.ds(0, half)], 1, prev_y))
    raw_a.wait_recv()
    own(after * per_y, half, (raw_up, ny_dev - 1))
    moves.append(move(after * per_y, got_up.at[pl.ds(0, half)], 2, next_y))
    raw_b.wait_recv()
    own(before * per_y + half, half, (raw_down, 1))
    moves.append(move(before * per_y + half, got_down.at[pl.ds(half, half)], 3, prev_y))
    own(y * per_y, per_y)

    for copy in moves:
        copy.wait_recv()

    def merge(i, carry):
        image[i] = weighted[y * per_y + i] + got_up[i] + got_down[i]
        return carry
    lax.fori_loop(0, per_y, merge, 0)

    finals = {}
    for dz in sorted(range(1, nz_dev), key=lambda d: -min(d, nz_dev - d)):
        target = lax.rem(z + dz, nz_dev)
        slot = nz_dev - dz - 1
        copy = remote(
            image.at[pl.ds(target * per_z, per_z)], arrived.at[slot],
            last_send.at[dz - 1], last_recv.at[slot], along[dz - 1],
        )
        copy.start()
        finals[dz] = copy
    result = image[pl.ds(z * per_z, per_z)]
    for dz, copy in finals.items():
        copy.wait_recv()
        result = result + arrived[nz_dev - dz - 1]
    out[...] = result

    for copy in finals.values():
        copy.wait_send()
    for copy in moves + [raw_a, raw_b]:
        copy.wait_send()
    pltpu.make_async_copy(others, others, small_send.at[0]).wait()
    pltpu.make_async_copy(rest, rest, small_send.at[1]).wait()

    @pl.when(depth < nd_dev - 1)
    def _():
        up.wait_send()

    @pl.when(depth > 0)
    def _():
        down.wait_send()


def solution(mesh):
    nd_dev = mesh.shape["depth"]
    ny_dev = ROWS_Y
    nz_dev = mesh.shape["shot"] // ny_dev

    def on_device(correlation, illumination, aperture):
        shots, nx, ny, nz = correlation.shape
        per_y = nx // ny_dev
        per_z = per_y // nz_dev
        half = per_y // 2
        dma = pltpu.SemaphoreType.DMA
        return pl.pallas_call(
            functools.partial(kernel, ny_dev, nz_dev, nd_dev),
            out_shape=jax.ShapeDtypeStruct((per_z, ny, nz), F32),
            in_specs=[
                pl.BlockSpec(memory_space=pltpu.SMEM),
                pl.BlockSpec(memory_space=pl.ANY),
                pl.BlockSpec(memory_space=pl.ANY),
            ],
            out_specs=pl.BlockSpec(memory_space=pltpu.VMEM),
            scratch_shapes=[
                pltpu.VMEM((shots, nx, ny, nz), F32),
                pltpu.VMEM((shots, nx, ny, nz), F32),
                pltpu.VMEM((shots, nx, ny, nz), F32),
                pltpu.VMEM((shots, ny, nz), F32),
                pltpu.VMEM((shots, ny, nz), F32),
                pltpu.VMEM((shots, ny, nz), F32),
                pltpu.VMEM((ny_dev * nd_dev, shots, nz), F32),
                pltpu.VMEM((nz_dev, shots, nz), F32),
                pltpu.VMEM((shots, half, ny, nz), F32),
                pltpu.VMEM((shots, half, ny, nz), F32),
                pltpu.VMEM((nx, ny, nz), F32),
                pltpu.VMEM((per_y, ny, nz), F32),
                pltpu.VMEM((per_y, ny, nz), F32),
                pltpu.VMEM((per_y, ny, nz), F32),
                pltpu.VMEM((nz_dev - 1, per_z, ny, nz), F32),
                dma((shots, PIECES, 2)),
                dma((2,)), dma((2,)), dma((2,)), dma((2,)),
                dma((2,)), dma((2,)), dma((4,)), dma((4,)),
                dma((nz_dev - 1,)), dma((nz_dev - 1,)),
            ],
            compiler_params=pltpu.CompilerParams(
                collective_id=0, has_side_effects=True, vmem_limit_bytes=67_043_328
            ),
        )(aperture, correlation, illumination)

    return jax.shard_map(
        on_device,
        mesh=mesh,
        in_specs=(P("shot", None, None, "depth"), P("shot", None, None, "depth"), P("shot", None)),
        out_specs=P("shot", None, "depth"),
        check_vma=False,
    )
```

time: 99.5 us -> 57 us (0.57); the launches traced: 97.5 us -> 56.3 us
  blocking collectives: 59.1 us -> 0 us
  Pallas kernels: 0 us -> 54.9 us
  other arithmetic: 17.1 us -> 0 us
  local copies, waits for them, and re-layouts: 13.4 us -> 1.38 us
  starting transfers between devices: 4.33 us -> 0 us
  waiting for transfers between devices: 2.81 us -> 0 us
    all_to_all x3 -> x0, blocking collectives: 59.1 us -> none  [the longest x1 30.5 us: summed_on_arrival(): lax.all_to_all(in_blocks(array, dim, devices), axis, 0, 0, tiled=True)]
    pallas_call x0 -> x1, Pallas kernels: none -> 54.9 us  [on_device(): pl.pallas_call(functools.partial(kernel, ny_dev, nz_dev, nd_dev), out_sha...]
    reduce_sum x4 -> x0, other arithmetic: 8.87 us -> none  [the longest x1 5.09 us: on_device(): local_energy = jnp.sum(filtered * filtered, axis=(1, 2, 3))]
    unnamed x4 -> x1, local copies, waits for them, and re-layouts: 10.1 us -> 1.38 us
    div x2 -> x0, other arithmetic: 4.63 us -> none  [the longest x1 4.53 us: on_device(): normalized = inside.astype(jnp.float32) * correlation / (illumination + 0.1)]
    ppermute x2 -> x0, starting transfers between devices: 4.33 us -> none  [the longest x1 2.41 us: padded_2(): lax.ppermute(lax.slice_in_dim(block, block.shape[dim] - width, None, axis...]
    ppermute x2 -> x0, waiting for transfers between devices: 2.81 us -> none  [the longest x1 2.81 us: padded_2(): lax.ppermute(lax.slice_in_dim(block, block.shape[dim] - width, None, axis...]
    concatenate x1 -> x0, other arithmetic: 2.24 us -> none  [padded_2(): block = jnp.concatenate([low, block, high], axis=dim)]
  transfers between devices with their start and end apart: 2 -> 0, of which waited for: 1 -> 0; matrix products, arithmetic and copies ran while one was open for 0% -> 0% of each run, Pallas kernels for 0% -> 0%
where the time goes in v1:
time: 57 us; the launch traced here: 56.3 us
  Pallas kernels  54.9 us (96%)
  local copies, waits for them, and re-layouts  1.38 us (2%)
    pallas_call x1, Pallas kernels, on_device(): pl.pallas_call(functools.partial(kernel, ny_dev, nz_dev, nd_dev), out_sha...  54.9 us
    unnamed x1, local copies, waits for them, and re-layouts  1.38 us

profile of v1, /device:TPU:4, one launch (start us, length us, event | category | flops | bytes accessed | tf_op | source)
XLA Modules:
  0.0 56.3 jit_solution(3165094823020791966)
XLA Ops:
  0.0 54.9 %shard_map.37 = f32[2,32,128]{2,1,0:T(8,128)} custom-call(s32[2,4]{1,0:T(2,128)} %box.1, f32[2,64,32,128]{3,2,1,0:T(8,128)} %corr.1, f32[2,64,32,128]{3,2,1,0:T(8,128)} %illum.1), custom_call_target="tpu_custom_call" | custom-call | tf_op jit(solution)/shard_map/pallas_call | solution.py:288
  54.9 1.4 %copy.5 = f32[2,32,128]{2,1,0:T(8,128)} copy(f32[2,32,128]{2,1,0:T(8,128)} %shard_map.37) | data formatting | bytes 65536

commit v2 on v1

v2 whole, which is shorter than its diff:
```python
import functools

import jax
import jax.numpy as jnp
from jax import lax
from jax.experimental import pallas as pl
from jax.experimental.pallas import tpu as pltpu
from jax.sharding import PartitionSpec as P

ROWS_Y = 4
PIECES = 4
UNROLL = 4
F32 = jnp.float32
MESH = pl.DeviceIdType.MESH


class Marks:
    def __init__(self):
        self.scope = None

    def __call__(self, name):
        if self.scope is not None:
            self.scope.__exit__(None, None, None)
            self.scope = None
        if name:
            self.scope = jax.named_scope(name)
            self.scope.__enter__()


def ring_order(count):
    return sorted(range(count), key=lambda d: (-min(d, count - d), d))


def kernel(
    ny_dev, nz_dev, nd_dev,
    box_hbm, corr, illum, out,
    box, corr_v, illum_v, norm, filt, edge, edge_low, edge_high, rim_v, side_v, mixed,
    energy, peaks, raw_out, raw_in, sent, got, image, arrived,
    box_sem, load_sem, edge_send, edge_recv, small_send, small_recv,
    raw_send, raw_recv, move_send, move_recv, last_send, last_recv,
):
    shots, nx, ny, nz = filt.shape
    mark = Marks()
    mark("p00_load_signal")
    shot, depth = lax.axis_index("shot"), lax.axis_index("depth")
    y, z = shot // nz_dev, shot % nz_dev
    per_y = nx // ny_dev
    group = nz // 4
    groups = nx // group

    box_load = pltpu.make_async_copy(box_hbm, box, box_sem)
    box_load.start()
    step = nx // PIECES
    loads = []
    for c in range(PIECES):
        piece = []
        for s in range(shots):
            rows = pl.ds(c * step, step)
            piece.append(pltpu.make_async_copy(corr.at[s, rows], corr_v.at[s, rows], load_sem.at[s, c, 0]))
            piece.append(pltpu.make_async_copy(illum.at[s, rows], illum_v.at[s, rows], load_sem.at[s, c, 1]))
        for copy in piece:
            copy.start()
        loads.append(piece)

    near = []
    for dy in range(ny_dev):
        for dd in range(nd_dev):
            if dy or dd:
                near.append({
                    "shot": lax.rem(y + dy, ny_dev) * nz_dev + z,
                    "depth": lax.rem(depth + dd, nd_dev),
                })
    along = [
        {"shot": y * nz_dev + lax.rem(z + dz, nz_dev), "depth": depth} for dz in range(1, nz_dev)
    ]
    barrier = pltpu.get_barrier_semaphore()
    for peer in near + along:
        pl.semaphore_signal(barrier, inc=1, device_id=peer, device_id_type=MESH)

    lane = lax.broadcasted_iota(jnp.int32, (ny, nz), 1)
    row = lax.broadcasted_iota(jnp.int32, (ny, nz), 0)
    first, last = lane == 0, lane == nz - 1
    ends = first | last
    top, bottom = row == 0, row == ny - 1
    column = lane // 4
    place = lax.rem(lane, 4)
    zero = jnp.zeros((ny, nz), F32)

    def beside_rows(here):
        return jnp.where(top, 0.0, pltpu.roll(here, 1, 0)) + jnp.where(bottom, 0.0, pltpu.roll(here, ny - 1, 0))

    box_load.wait()
    mark("p01_filter")
    strips = [((row >= box[s, 2]) & (row < box[s, 3])).astype(F32) for s in range(shots)]
    bounds = [(box[s, 0], box[s, 1]) for s in range(shots)]
    for s in range(shots):
        norm[s, 0] = zero
        norm[s, nx + 1] = zero

    def normalize(k, packs):
        packs = list(packs)
        for s in range(shots):
            for j in range(UNROLL):
                x = k * UNROLL + j
                inside = jnp.where((x >= bounds[s][0]) & (x < bounds[s][1]), 1.0, 0.0).astype(F32)
                value = (strips[s] * inside) * corr_v[s, x] / (illum_v[s, x] + 0.1)
                norm[s, x + 1] = value
                turned = pltpu.roll(value, lax.rem(4 * x + 2, nz), 1)
                packs[s] = jnp.where(column == lax.rem(x, group), turned, packs[s])
        return tuple(packs)

    def filter_block(k, sums):
        sums = list(sums)
        for s in range(shots):
            rows = [norm[s, k * UNROLL + i] for i in range(UNROLL + 2)]
            for j in range(UNROLL):
                here = rows[j + 1]
                beside = rows[j] + rows[j + 2] + beside_rows(here)
                beside = beside + jnp.where(first, 0.0, pltpu.roll(here, 1, 1))
                beside = beside + jnp.where(last, 0.0, pltpu.roll(here, nz - 1, 1))
                value = 6.0 * here - beside
                filt[s, k * UNROLL + j] = value
                sums[s] = sums[s] + value * value
        return tuple(sums)

    blocks = nx // UNROLL
    per_piece = step // UNROLL
    packs, sums, packed = (zero,) * shots, (zero,) * shots, []
    for c in range(PIECES):
        for copy in loads[c]:
            copy.wait()
        begin = c * per_piece
        if c == 0:
            for k in range(2):
                packs = normalize(k, packs)
            begin = 2

        def body(k, carry):
            packs, sums = carry
            sums = filter_block(k - 2, sums)
            return normalize(k, packs), sums

        packs, sums = lax.fori_loop(begin, (c + 1) * per_piece, body, (packs, sums))
        if (c + 1) * step % group == 0:
            packed.append(packs)
            packs = (zero,) * shots
    for k in (blocks - 2, blocks - 1):
        sums = filter_block(k, sums)

    mark("p02_pack")
    inner = (place == 1) | (place == 2)
    for s in range(shots):
        parts = [packed[g][s] for g in range(groups)]
        edge[s] = jnp.where(inner, parts[0], pltpu.roll(parts[1], 2, 1))
        backs = [pltpu.roll(part, 4, 1) for part in parts]
        aheads = [pltpu.roll(part, nz - 4, 1) for part in parts]
        for g, part in enumerate(parts):
            back = jnp.where(lane < 4, backs[g - 1] if g else 0.0, backs[g])
            ahead = jnp.where(lane >= nz - 4, aheads[g + 1] if g < groups - 1 else 0.0, aheads[g])
            deep = jnp.where(place == 1, pltpu.roll(part, 1, 1), pltpu.roll(part, nz - 1, 1))
            rim_v[s, g] = 6.0 * part - (back + ahead + beside_rows(part) + deep)

    mark("p02b_barrier")
    pl.semaphore_wait(barrier, len(near) + len(along))
    mark("p03_halo")

    def remote(src, dst, send, recv, peer):
        return pltpu.make_async_remote_copy(
            src_ref=src, dst_ref=dst, send_sem=send, recv_sem=recv, device_id=peer, device_id_type=MESH
        )

    up = remote(edge, edge_low, edge_send.at[0], edge_recv.at[0], {"shot": shot, "depth": lax.rem(depth + 1, nd_dev)})
    down = remote(edge, edge_high, edge_send.at[1], edge_recv.at[1], {"shot": shot, "depth": lax.rem(depth + nd_dev - 1, nd_dev)})

    @pl.when(depth < nd_dev - 1)
    def _():
        up.start()

    @pl.when(depth > 0)
    def _():
        down.start()

    @pl.when(depth == 0)
    def _():
        edge_low[...] = jnp.zeros_like(edge_low)

    @pl.when(depth == nd_dev - 1)
    def _():
        edge_high[...] = jnp.zeros_like(edge_high)

    @pl.when(depth > 0)
    def _():
        up.wait_recv()

    @pl.when(depth < nd_dev - 1)
    def _():
        down.wait_recv()

    mark("p04_energy")
    for s in range(shots):
        total = jnp.where(ends, 0.0, sums[s])
        high, low = edge_high[s], edge_low[s]
        for g in range(groups):
            side = jnp.where(
                place == 1,
                pltpu.roll(high, (nz - 1 - 2 * g) % nz, 1),
                pltpu.roll(low, (nz + 1 - 2 * g) % nz, 1),
            )
            side_v[s, g] = side
            rim = rim_v[s, g] - side
            total = total + jnp.where(inner, rim * rim, 0.0)
        energy[0, s : s + 1] = jnp.sum(total, axis=0, keepdims=True)

    for i, peer in enumerate(near):
        dy, dd = (i + 1) // nd_dev, (i + 1) % nd_dev
        slot = ((ny_dev - dy) % ny_dev) * nd_dev + (nd_dev - dd) % nd_dev
        remote(energy.at[0], energy.at[slot], small_send.at[0], small_recv.at[0], peer).start()

    mark("p05_raw")
    after = lax.rem(y + 1, ny_dev)
    before = lax.rem(y + ny_dev - 1, ny_dev)
    across = lax.rem(y + ny_dev // 2, ny_dev)
    next_y = {"shot": after * nz_dev + z, "depth": depth}
    prev_y = {"shot": before * nz_dev + z, "depth": depth}

    def ends_of(packed_side, x):
        return jnp.where(ends, pltpu.roll(packed_side, lax.rem(2 * nz - 2 - 4 * lax.rem(x, group), nz), 1), 0.0)

    def raw_body(i, carry):
        for s in range(shots):
            side = side_v[s, across * per_y // group]
            for way in range(2):
                x = across * per_y + 2 * i + way
                raw_out[way, s, i] = filt[s, x] - ends_of(side, x)
        return carry

    lax.fori_loop(0, nz_dev, raw_body, 0)
    raws = [remote(raw_out.at[i], raw_in.at[i], raw_send.at[i], raw_recv.at[i], (next_y, prev_y)[i]) for i in range(2)]
    for copy in raws:
        copy.start()

    mark("p06_wait_energy")
    others = energy.at[pl.ds(1, len(near))]
    pltpu.make_async_copy(others, others, small_recv.at[0]).wait()
    mark("p07_means")
    cells = nx * ny * nz * nd_dev
    means = []
    for dy in range(ny_dev):
        both = jnp.sum(energy[dy * nd_dev : (dy + 1) * nd_dev], axis=0)
        means.append(jnp.broadcast_to(jnp.sum(both, axis=1, keepdims=True) / cells, (shots, nz)))
    peaks[0] = functools.reduce(jnp.maximum, means)
    for i, peer in enumerate(along):
        remote(peaks.at[0], peaks.at[nz_dev - 1 - i], small_send.at[1], small_recv.at[1], peer).start()
    rest = peaks.at[pl.ds(1, len(along))]
    mark("p08_wait_peak")
    pltpu.make_async_copy(rest, rest, small_recv.at[1]).wait()
    mark("p09_weights")
    peak = jnp.max(jnp.max(peaks[...], axis=0), axis=0, keepdims=True)
    scale = 1.0 / float(shots * ny_dev * nz_dev) ** 0.5
    weights = [scale / jnp.sqrt(mean + 0.5 * peak + 1.0) for mean in means]

    def weight(dy, s):
        return jnp.broadcast_to(weights[dy][s : s + 1], (ny, nz))

    for g in range(groups):
        mixed[g] = sum(weight(0, s) * side_v[s, g] for s in range(shots))

    def own(x):
        total = sum(weight(0, s) * filt[s, x] for s in range(shots))
        return total - ends_of(mixed[x // group], x)

    mark("p10_ysend")
    for copy in raws:
        copy.wait_recv()
    order = ring_order(nz_dev)
    moves = []
    for i, dz in enumerate(order):
        target = lax.rem(z + dz, nz_dev)
        for way, (peer, place_y, origin) in enumerate(((next_y, after, ny_dev - 1), (prev_y, before, 1))):
            for j in range(2):
                value = own(place_y * per_y + 2 * target + j)
                if j == way:
                    value = value + sum(weight(origin, s) * raw_in[way, s, target] for s in range(shots))
                sent[way, i, j] = value
            copy = remote(sent.at[way, i], got.at[way, i], move_send.at[way, i], move_recv.at[way, i], peer)
            copy.start()
            moves.append(copy)
    for i, dz in enumerate(order):
        target = lax.rem(z + dz, nz_dev)
        for j in range(2):
            image[i, j] = own(y * per_y + 2 * target + j)

    mark("p11_zsend")
    finals = []
    for i, dz in enumerate(order):
        for way in range(2):
            moves[2 * i + way].wait_recv()
        value = image[i] + got[0, i] + got[1, i]
        image[i] = value
        if dz:
            slot = nz_dev - 1 - dz
            copy = remote(image.at[i], arrived.at[slot], last_send.at[slot], last_recv.at[slot], along[dz - 1])
            copy.start()
            finals.append((copy, slot))
    mark("p12_zwait")
    result = value
    for copy, slot in finals:
        copy.wait_recv()
        result = result + arrived[slot]
    out[...] = result

    mark("p13_tail")
    for copy, _ in finals:
        copy.wait_send()
    for copy in moves + raws:
        copy.wait_send()
    pltpu.make_async_copy(others, others, small_send.at[0]).wait()
    pltpu.make_async_copy(rest, rest, small_send.at[1]).wait()

    @pl.when(depth < nd_dev - 1)
    def _():
        up.wait_send()

    @pl.when(depth > 0)
    def _():
        down.wait_send()

    mark(None)


def solution(mesh):
    nd_dev = mesh.shape["depth"]
    ny_dev = ROWS_Y
    nz_dev = mesh.shape["shot"] // ny_dev

    def on_device(correlation, illumination, aperture):
        shots, nx, ny, nz = correlation.shape
        per_z = nx // ny_dev // nz_dev
        assert per_z == 2 and nz == 128 and nx == 64
        dma = pltpu.SemaphoreType.DMA
        field = (ny, nz)
        return pl.pallas_call(
            functools.partial(kernel, ny_dev, nz_dev, nd_dev),
            out_shape=jax.ShapeDtypeStruct((per_z, ny, nz), F32),
            in_specs=[pl.BlockSpec(memory_space=pl.ANY)] * 3,
            out_specs=pl.BlockSpec(memory_space=pltpu.VMEM),
            scratch_shapes=[
                pltpu.SMEM((shots, 4), jnp.int32),
                pltpu.VMEM((shots, nx, *field), F32),
                pltpu.VMEM((shots, nx, *field), F32),
                pltpu.VMEM((shots, nx + 2, *field), F32),
                pltpu.VMEM((shots, nx, *field), F32),
                pltpu.VMEM((shots, *field), F32),
                pltpu.VMEM((shots, *field), F32),
                pltpu.VMEM((shots, *field), F32),
                pltpu.VMEM((shots, 2, *field), F32),
                pltpu.VMEM((shots, 2, *field), F32),
                pltpu.VMEM((2, *field), F32),
                pltpu.VMEM((ny_dev * nd_dev, shots, nz), F32),
                pltpu.VMEM((nz_dev, shots, nz), F32),
                pltpu.VMEM((2, shots, nz_dev, *field), F32),
                pltpu.VMEM((2, shots, nz_dev, *field), F32),
                pltpu.VMEM((2, nz_dev, per_z, *field), F32),
                pltpu.VMEM((2, nz_dev, per_z, *field), F32),
                pltpu.VMEM((nz_dev, per_z, *field), F32),
                pltpu.VMEM((nz_dev - 1, per_z, *field), F32),
                dma, dma((shots, PIECES, 2)),
                dma((2,)), dma((2,)), dma((2,)), dma((2,)),
                dma((2,)), dma((2,)), dma((2, nz_dev)), dma((2, nz_dev)),
                dma((nz_dev - 1,)), dma((nz_dev - 1,)),
            ],
            compiler_params=pltpu.CompilerParams(
                collective_id=0, has_side_effects=True, vmem_limit_bytes=67_043_328 - (256 << 10)
            ),
        )(aperture, correlation, illumination)

    return jax.shard_map(
        on_device,
        mesh=mesh,
        in_specs=(P("shot", None, None, "depth"), P("shot", None, None, "depth"), P("shot", None)),
        out_specs=P("shot", None, "depth"),
        check_vma=False,
    )
```

time: 57 us -> 35.2 us (0.62)
  Pallas kernels: 54.9 us -> 33.1 us
    pallas_call x1, Pallas kernels: 54.9 us -> 33.1 us  [on_device(): pl.pallas_call(functools.partial(kernel, ny_dev, nz_dev, nd_dev), out_sha...]
where the time goes in v2:
time: 35.2 us; the launch traced here: 34.5 us
  Pallas kernels  33.1 us (94%)
  local copies, waits for them, and re-layouts  1.38 us (4%)
    pallas_call x1, Pallas kernels, on_device(): pl.pallas_call(functools.partial(kernel, ny_dev, nz_dev, nd_dev), out_sha...  33.1 us
    unnamed x1, local copies, waits for them, and re-layouts  1.38 us

profile of v2, /device:TPU:4, one launch (start us, length us, event | category | flops | bytes accessed | tf_op | source)
XLA Modules:
  0.0 34.5 jit_solution(13221971884782201273)
XLA Ops:
  0.0 33.1 %shard_map.37 = f32[2,32,128]{2,1,0:T(8,128)} custom-call(s32[2,4]{1,0:T(2,128)} %box_hbm.1, f32[2,64,32,128]{3,2,1,0:T(8,128)} %corr.1, f32[2,64,32,128]{3,2,1,0:T(8,128)} %illum.1), custom_call_target="tpu_custom_call" | custom-call | tf_op jit(solution)/shard_map/pallas_call | solution.py:342
  33.1 1.4 %copy.5 = f32[2,32,128]{2,1,0:T(8,128)} copy(f32[2,32,128]{2,1,0:T(8,128)} %shard_map.37) | data formatting | bytes 65536

commit v3 on v2

--- a/solution.py
+++ b/solution.py
@@ -28,14 +28,14 @@
 
 
 def ring_order(count):
-    return sorted(range(count), key=lambda d: (-min(d, count - d), d))
+    return sorted((d for d in range(count) if 2 * d != count), key=lambda d: (-min(d, count - d), d))
 
 
 def kernel(
     ny_dev, nz_dev, nd_dev,
     box_hbm, corr, illum, out,
-    box, corr_v, illum_v, norm, filt, edge, edge_low, edge_high, rim_v, side_v, mixed,
-    energy, peaks, raw_out, raw_in, sent, got, image, arrived,
+    box, corr_v, illum_v, norm, filt, edge, edge_low, edge_high, rim_v, wrap_v, side_v, mixed,
+    energy, peaks, raw_out, raw_in, cross_out, cross_in, sent, got, image, arrived,
     box_sem, load_sem, edge_send, edge_recv, small_send, small_recv,
     raw_send, raw_recv, move_send, move_recv, last_send, last_recv,
 ):
@@ -73,14 +73,18 @@
     along = [
         {"shot": y * nz_dev + lax.rem(z + dz, nz_dev), "depth": depth} for dz in range(1, nz_dev)
     ]
+    after, before, across = (lax.rem(y + d, ny_dev) for d in (1, ny_dev - 1, ny_dev // 2))
+    corners = [
+        {"shot": side * nz_dev + lax.rem(z + d, nz_dev), "depth": depth}
+        for side, d in ((after, 1), (before, nz_dev - 1))
+    ]
     barrier = pltpu.get_barrier_semaphore()
-    for peer in near + along:
+    for peer in near + along + corners:
         pl.semaphore_signal(barrier, inc=1, device_id=peer, device_id_type=MESH)
 
     lane = lax.broadcasted_iota(jnp.int32, (ny, nz), 1)
     row = lax.broadcasted_iota(jnp.int32, (ny, nz), 0)
-    first, last = lane == 0, lane == nz - 1
-    ends = first | last
+    ends = (lane == 0) | (lane == nz - 1)
     top, bottom = row == 0, row == ny - 1
     column = lane // 4
     place = lax.rem(lane, 4)
@@ -116,8 +120,7 @@
             for j in range(UNROLL):
                 here = rows[j + 1]
                 beside = rows[j] + rows[j + 2] + beside_rows(here)
-                beside = beside + jnp.where(first, 0.0, pltpu.roll(here, 1, 1))
-                beside = beside + jnp.where(last, 0.0, pltpu.roll(here, nz - 1, 1))
+                beside = beside + pltpu.roll(here, 1, 1) + pltpu.roll(here, nz - 1, 1)
                 value = 6.0 * here - beside
                 filt[s, k * UNROLL + j] = value
                 sums[s] = sums[s] + value * value
@@ -157,11 +160,13 @@
         for g, part in enumerate(parts):
             back = jnp.where(lane < 4, backs[g - 1] if g else 0.0, backs[g])
             ahead = jnp.where(lane >= nz - 4, aheads[g + 1] if g < groups - 1 else 0.0, aheads[g])
-            deep = jnp.where(place == 1, pltpu.roll(part, 1, 1), pltpu.roll(part, nz - 1, 1))
+            lower, higher = pltpu.roll(part, 1, 1), pltpu.roll(part, nz - 1, 1)
+            deep = jnp.where(place == 1, lower, higher)
             rim_v[s, g] = 6.0 * part - (back + ahead + beside_rows(part) + deep)
+            wrap_v[s, g] = jnp.where(place == 1, higher, lower)
 
     mark("p02b_barrier")
-    pl.semaphore_wait(barrier, len(near) + len(along))
+    pl.semaphore_wait(barrier, len(near) + len(along) + len(corners))
     mark("p03_halo")
 
     def remote(src, dst, send, recv, peer):
@@ -206,7 +211,7 @@
                 pltpu.roll(high, (nz - 1 - 2 * g) % nz, 1),
                 pltpu.roll(low, (nz + 1 - 2 * g) % nz, 1),
             )
-            side_v[s, g] = side
+            side_v[s, g] = side - wrap_v[s, g]
             rim = rim_v[s, g] - side
             total = total + jnp.where(inner, rim * rim, 0.0)
         energy[0, s : s + 1] = jnp.sum(total, axis=0, keepdims=True)
@@ -217,27 +222,44 @@
         remote(energy.at[0], energy.at[slot], small_send.at[0], small_recv.at[0], peer).start()
 
     mark("p05_raw")
-    after = lax.rem(y + 1, ny_dev)
-    before = lax.rem(y + ny_dev - 1, ny_dev)
-    across = lax.rem(y + ny_dev // 2, ny_dev)
     next_y = {"shot": after * nz_dev + z, "depth": depth}
     prev_y = {"shot": before * nz_dev + z, "depth": depth}
+    next_z, prev_z = along[0], along[-1]
+    order = ring_order(nz_dev)
+    owners = [lax.rem(z + dz, nz_dev) for dz in order]
+    opposite = lax.rem(z + nz_dev // 2, nz_dev)
 
     def ends_of(packed_side, x):
         return jnp.where(ends, pltpu.roll(packed_side, lax.rem(2 * nz - 2 - 4 * lax.rem(x, group), nz), 1), 0.0)
 
-    def raw_body(i, carry):
+    def raw(s, x):
+        return filt[s, x] - ends_of(side_v[s, x // group], x)
+
+    chips = (y, after, before, across)
+    for way in range(2):
         for s in range(shots):
-            side = side_v[s, across * per_y // group]
-            for way in range(2):
-                x = across * per_y + 2 * i + way
-                raw_out[way, s, i] = filt[s, x] - ends_of(side, x)
-        return carry
-
-    lax.fori_loop(0, nz_dev, raw_body, 0)
-    raws = [remote(raw_out.at[i], raw_in.at[i], raw_send.at[i], raw_recv.at[i], (next_y, prev_y)[i]) for i in range(2)]
+            for i, chip in enumerate(chips):
+                cross_out[way, s, i] = raw(s, chip * per_y + 2 * opposite + way)
+    raws = []
+    for way in range(2):
+        straight, corner = pl.ds(0, 3), pl.ds(3, 1)
+        raws.append(remote(
+            cross_out.at[way, :, straight], cross_in.at[way, :, straight],
+            raw_send.at[0, way], raw_recv.at[0, way], (next_z, prev_z)[way],
+        ))
+        raws.append(remote(
+            cross_out.at[way, :, corner], cross_in.at[way, :, corner],
+            raw_send.at[1, way], raw_recv.at[1, way], corners[way],
+        ))
     for copy in raws:
         copy.start()
+    for way in range(2):
+        for s in range(shots):
+            for i, owner in enumerate(owners):
+                raw_out[way, s, i] = raw(s, across * per_y + 2 * owner + way)
+        copy = remote(raw_out.at[way], raw_in.at[way], raw_send.at[2, way], raw_recv.at[2, way], (next_y, prev_y)[way])
+        copy.start()
+        raws.append(copy)
 
     mark("p06_wait_energy")
     others = energy.at[pl.ds(1, len(near))]
@@ -248,7 +270,8 @@
     for dy in range(ny_dev):
         both = jnp.sum(energy[dy * nd_dev : (dy + 1) * nd_dev], axis=0)
         means.append(jnp.broadcast_to(jnp.sum(both, axis=1, keepdims=True) / cells, (shots, nz)))
-    peaks[0] = functools.reduce(jnp.maximum, means)
+    for dy in range(ny_dev):
+        peaks[0, dy * shots : (dy + 1) * shots] = means[dy]
     for i, peer in enumerate(along):
         remote(peaks.at[0], peaks.at[nz_dev - 1 - i], small_send.at[1], small_recv.at[1], peer).start()
     rest = peaks.at[pl.ds(1, len(along))]
@@ -257,38 +280,43 @@
     mark("p09_weights")
     peak = jnp.max(jnp.max(peaks[...], axis=0), axis=0, keepdims=True)
     scale = 1.0 / float(shots * ny_dev * nz_dev) ** 0.5
-    weights = [scale / jnp.sqrt(mean + 0.5 * peak + 1.0) for mean in means]
-
-    def weight(dy, s):
-        return jnp.broadcast_to(weights[dy][s : s + 1], (ny, nz))
+    weights = {dz: scale / jnp.sqrt(peaks[dz] + 0.5 * peak + 1.0) for dz in (0, 1, nz_dev - 1)}
+
+    def weight(dy, dz, s):
+        return jnp.broadcast_to(weights[dz][dy * shots + s : dy * shots + s + 1], (ny, nz))
+
+    def blend(dy, dz, value):
+        return sum(weight(dy, dz, s) * value(s) for s in range(shots))
 
     for g in range(groups):
-        mixed[g] = sum(weight(0, s) * side_v[s, g] for s in range(shots))
-
-    def own(x):
-        total = sum(weight(0, s) * filt[s, x] for s in range(shots))
-        return total - ends_of(mixed[x // group], x)
+        mixed[g] = blend(0, 0, lambda s: side_v[s, g])
 
     mark("p10_ysend")
     for copy in raws:
         copy.wait_recv()
-    order = ring_order(nz_dev)
+
+    def share(i, chip, j):
+        x = chips[chip] * per_y + 2 * owners[i] + j
+        total = blend(0, 0, lambda s: filt[s, x]) - ends_of(mixed[x // group], x)
+        if chip and j == chip - 1:
+            total = total + blend((ny_dev - 1, 1)[j], 0, lambda s: raw_in[j, s, i])
+        if order[i] == (nz_dev // 2 - 1, nz_dev // 2 + 1)[j]:
+            total = total + blend(0, (nz_dev - 1, 1)[j], lambda s: cross_in[j, s, chip])
+            if chip and j == chip - 1:
+                total = total + blend((ny_dev - 1, 1)[j], (nz_dev - 1, 1)[j], lambda s: cross_in[j, s, 3])
+        return total
+
     moves = []
-    for i, dz in enumerate(order):
-        target = lax.rem(z + dz, nz_dev)
-        for way, (peer, place_y, origin) in enumerate(((next_y, after, ny_dev - 1), (prev_y, before, 1))):
+    for i in range(len(order)):
+        for way, peer in enumerate((next_y, prev_y)):
             for j in range(2):
-                value = own(place_y * per_y + 2 * target + j)
-                if j == way:
-                    value = value + sum(weight(origin, s) * raw_in[way, s, target] for s in range(shots))
-                sent[way, i, j] = value
+                sent[way, i, j] = share(i, 1 + way, j)
             copy = remote(sent.at[way, i], got.at[way, i], move_send.at[way, i], move_recv.at[way, i], peer)
             copy.start()
             moves.append(copy)
-    for i, dz in enumerate(order):
-        target = lax.rem(z + dz, nz_dev)
+    for i in range(len(order)):
         for j in range(2):
-            image[i, j] = own(y * per_y + 2 * target + j)
+            image[i, j] = share(i, 0, j)
 
     mark("p11_zsend")
     finals = []
@@ -298,19 +326,18 @@
         value = image[i] + got[0, i] + got[1, i]
         image[i] = value
         if dz:
-            slot = nz_dev - 1 - dz
-            copy = remote(image.at[i], arrived.at[slot], last_send.at[slot], last_recv.at[slot], along[dz - 1])
+            copy = remote(image.at[i], arrived.at[i], last_send.at[i], last_recv.at[i], along[dz - 1])
             copy.start()
-            finals.append((copy, slot))
+            finals.append(copy)
     mark("p12_zwait")
     result = value
-    for copy, slot in finals:
+    for i, copy in enumerate(finals):
         copy.wait_recv()
-        result = result + arrived[slot]
+        result = result + arrived[i]
     out[...] = result
 
     mark("p13_tail")
-    for copy, _ in finals:
+    for copy in finals:
         copy.wait_send()
     for copy in moves + raws:
         copy.wait_send()
@@ -339,6 +366,7 @@
         assert per_z == 2 and nz == 128 and nx == 64
         dma = pltpu.SemaphoreType.DMA
         field = (ny, nz)
+        chunks = len(ring_order(nz_dev))
         return pl.pallas_call(
             functools.partial(kernel, ny_dev, nz_dev, nd_dev),
             out_shape=jax.ShapeDtypeStruct((per_z, ny, nz), F32),
@@ -355,24 +383,27 @@
                 pltpu.VMEM((shots, *field), F32),
                 pltpu.VMEM((shots, 2, *field), F32),
                 pltpu.VMEM((shots, 2, *field), F32),
+                pltpu.VMEM((shots, 2, *field), F32),
                 pltpu.VMEM((2, *field), F32),
                 pltpu.VMEM((ny_dev * nd_dev, shots, nz), F32),
-                pltpu.VMEM((nz_dev, shots, nz), F32),
-                pltpu.VMEM((2, shots, nz_dev, *field), F32),
-                pltpu.VMEM((2, shots, nz_dev, *field), F32),
-                pltpu.VMEM((2, nz_dev, per_z, *field), F32),
-                pltpu.VMEM((2, nz_dev, per_z, *field), F32),
-                pltpu.VMEM((nz_dev, per_z, *field), F32),
-                pltpu.VMEM((nz_dev - 1, per_z, *field), F32),
+                pltpu.VMEM((nz_dev, ny_dev * shots, nz), F32),
+                pltpu.VMEM((2, shots, chunks, *field), F32),
+                pltpu.VMEM((2, shots, chunks, *field), F32),
+                pltpu.VMEM((2, shots, 4, *field), F32),
+                pltpu.VMEM((2, shots, 4, *field), F32),
+                pltpu.VMEM((2, chunks, per_z, *field), F32),
+                pltpu.VMEM((2, chunks, per_z, *field), F32),
+                pltpu.VMEM((chunks, per_z, *field), F32),
+                pltpu.VMEM((chunks - 1, per_z, *field), F32),
                 dma, dma((shots, PIECES, 2)),
                 dma((2,)), dma((2,)), dma((2,)), dma((2,)),
-                dma((2,)), dma((2,)), dma((2, nz_dev)), dma((2, nz_dev)),
-                dma((nz_dev - 1,)), dma((nz_dev - 1,)),
+                dma((3, 2)), dma((3, 2)), dma((2, chunks)), dma((2, chunks)),
+                dma((chunks - 1,)), dma((chunks - 1,)),
             ],
             compiler_params=pltpu.CompilerParams(
-                collective_id=0, has_side_effects=True, vmem_limit_bytes=67_043_328 - (256 << 10)
+                collective_id=0, has_side_effects=True, vmem_limit_bytes=32 << 20
             ),
-        )(aperture, correlation, illumination)
+        )(*(pltpu.with_memory_space_constraint(a, pltpu.HBM) for a in (aperture, correlation, illumination)))
 
     return jax.shard_map(
         on_device,

time: 35.2 us -> 32.8 us (0.932)
  the two profiles are of different devices: /device:TPU:4 before, /device:TPU:8 now
where the time goes in v3:
time: 32.8 us; the launch traced here: 32.7 us
  Pallas kernels  32.1 us (98%)
  local copies, waits for them, and re-layouts  0.62 us (2%)
    pallas_call x1, Pallas kernels, on_device(): pl.pallas_call(functools.partial(kernel, ny_dev, nz_dev, nd_dev), out_sha...  32.1 us

profile of v3, /device:TPU:8, one launch (start us, length us, event | category | flops | bytes accessed | tf_op | source)
XLA Modules:
  0.0 32.7 jit_solution(7284785508287537295)
XLA Ops:
  0.0 32.1 %shard_map.37 = f32[2,32,128]{2,1,0:T(8,128)S(1)} custom-call(s32[2,4]{1,0:T(2,128)} %box_hbm.1, f32[2,64,32,128]{3,2,1,0:T(8,128)} %corr.1, f32[2,64,32,128]{3,2,1,0:T(8,128)} %illum.1), custom_call_target="tpu_custom_call" | custom-call | tf_op jit(solution)/shard_map/pallas_call | solution.py:370
  32.1 0.6 %copy.5 = f32[2,32,128]{2,1,0:T(8,128)} copy(f32[2,32,128]{2,1,0:T(8,128)S(1)} %shard_map.37) | data formatting | bytes 65536

commit v4 on v3

--- a/solution.py
+++ b/solution.py
@@ -9,7 +9,10 @@
 
 ROWS_Y = 4
 PIECES = 4
-UNROLL = 4
+NORM_ROWS = 16
+FILTER_ROWS = 16
+PAD = 8
+ORDER = (0, 1, 2, 3, 7, 6, 5, 4)
 F32 = jnp.float32
 MESH = pl.DeviceIdType.MESH
 
@@ -27,15 +30,11 @@
             self.scope.__enter__()
 
 
-def ring_order(count):
-    return sorted((d for d in range(count) if 2 * d != count), key=lambda d: (-min(d, count - d), d))
-
-
 def kernel(
     ny_dev, nz_dev, nd_dev,
     box_hbm, corr, illum, out,
     box, corr_v, illum_v, norm, filt, edge, edge_low, edge_high, rim_v, wrap_v, side_v, mixed,
-    energy, peaks, raw_out, raw_in, cross_out, cross_in, sent, got, image, arrived,
+    energy, peaks, raw_out, raw_in, cross_out, cross_in, cross_sum, sent, got, image, arrived,
     box_sem, load_sem, edge_send, edge_recv, small_send, small_recv,
     raw_send, raw_recv, move_send, move_recv, last_send, last_recv,
 ):
@@ -58,9 +57,9 @@
             rows = pl.ds(c * step, step)
             piece.append(pltpu.make_async_copy(corr.at[s, rows], corr_v.at[s, rows], load_sem.at[s, c, 0]))
             piece.append(pltpu.make_async_copy(illum.at[s, rows], illum_v.at[s, rows], load_sem.at[s, c, 1]))
-        for copy in piece:
-            copy.start()
         loads.append(piece)
+    for copy in loads[0]:
+        copy.start()
 
     near = []
     for dy in range(ny_dev):
@@ -81,6 +80,9 @@
     barrier = pltpu.get_barrier_semaphore()
     for peer in near + along + corners:
         pl.semaphore_signal(barrier, inc=1, device_id=peer, device_id_type=MESH)
+    for piece in loads[1:]:
+        for copy in piece:
+            copy.start()
 
     lane = lax.broadcasted_iota(jnp.int32, (ny, nz), 1)
     row = lax.broadcasted_iota(jnp.int32, (ny, nz), 0)
@@ -93,22 +95,32 @@
     def beside_rows(here):
         return jnp.where(top, 0.0, pltpu.roll(here, 1, 0)) + jnp.where(bottom, 0.0, pltpu.roll(here, ny - 1, 0))
 
-    box_load.wait()
-    mark("p01_filter")
     strips = [((row >= box[s, 2]) & (row < box[s, 3])).astype(F32) for s in range(shots)]
     bounds = [(box[s, 0], box[s, 1]) for s in range(shots)]
+    blank = jnp.zeros((PAD, nz), F32)
+
+    def clear(x, carry):
+        for s in range(shots):
+            norm[s, x, :PAD] = blank
+            norm[s, x, PAD + ny :] = blank
+        return carry
+
+    lax.fori_loop(1, nx + 1, clear, 0)
     for s in range(shots):
-        norm[s, 0] = zero
-        norm[s, nx + 1] = zero
+        for x in (0, nx + 1):
+            norm[s, x] = jnp.zeros((ny + 2 * PAD, nz), F32)
+    box_load.wait()
+    strips = [((row >= box[s, 2]) & (row < box[s, 3])).astype(F32) for s in range(shots)]
+    bounds = [(box[s, 0], box[s, 1]) for s in range(shots)]
 
     def normalize(k, packs):
         packs = list(packs)
         for s in range(shots):
-            for j in range(UNROLL):
-                x = k * UNROLL + j
+            for j in range(NORM_ROWS):
+                x = k * NORM_ROWS + j
                 inside = jnp.where((x >= bounds[s][0]) & (x < bounds[s][1]), 1.0, 0.0).astype(F32)
                 value = (strips[s] * inside) * corr_v[s, x] / (illum_v[s, x] + 0.1)
-                norm[s, x + 1] = value
+                norm[s, x + 1, PAD : PAD + ny] = value
                 turned = pltpu.roll(value, lax.rem(4 * x + 2, nz), 1)
                 packs[s] = jnp.where(column == lax.rem(x, group), turned, packs[s])
         return tuple(packs)
@@ -116,45 +128,68 @@
     def filter_block(k, sums):
         sums = list(sums)
         for s in range(shots):
-            rows = [norm[s, k * UNROLL + i] for i in range(UNROLL + 2)]
-            for j in range(UNROLL):
+            base = k * FILTER_ROWS
+            rows = [norm[s, base + i, PAD : PAD + ny] for i in range(FILTER_ROWS + 2)]
+            for j in range(FILTER_ROWS):
                 here = rows[j + 1]
-                beside = rows[j] + rows[j + 2] + beside_rows(here)
+                beside = rows[j] + rows[j + 2] + (norm[s, base + j + 1, pl.ds(PAD - 1 + lax.min(k, 0), ny)] + norm[s, base + j + 1, pl.ds(PAD + 1 + lax.min(k, 0), ny)])
                 beside = beside + pltpu.roll(here, 1, 1) + pltpu.roll(here, nz - 1, 1)
                 value = 6.0 * here - beside
-                filt[s, k * UNROLL + j] = value
+                filt[s, base + j] = value
                 sums[s] = sums[s] + value * value
         return tuple(sums)
 
-    blocks = nx // UNROLL
-    per_piece = step // UNROLL
-    packs, sums, packed = (zero,) * shots, (zero,) * shots, []
+    packs, packed = (zero,) * shots, []
     for c in range(PIECES):
+        mark(f"p01_w{c}")
         for copy in loads[c]:
             copy.wait()
-        begin = c * per_piece
-        if c == 0:
-            for k in range(2):
-                packs = normalize(k, packs)
-            begin = 2
-
-        def body(k, carry):
-            packs, sums = carry
-            sums = filter_block(k - 2, sums)
-            return normalize(k, packs), sums
-
-        packs, sums = lax.fori_loop(begin, (c + 1) * per_piece, body, (packs, sums))
+        mark(f"p01_x{c}")
+        blocks = step // NORM_ROWS
+        packs = lax.fori_loop(c * blocks, (c + 1) * blocks, normalize, packs)
         if (c + 1) * step % group == 0:
             packed.append(packs)
             packs = (zero,) * shots
-    for k in (blocks - 2, blocks - 1):
-        sums = filter_block(k, sums)
 
     mark("p02_pack")
     inner = (place == 1) | (place == 2)
     for s in range(shots):
+        edge[s] = jnp.where(inner, packed[0][s], pltpu.roll(packed[1][s], 2, 1))
+
+    mark("p02b_barrier")
+    pl.semaphore_wait(barrier, len(near) + len(along) + len(corners))
+    mark("p03_halo")
+
+    def remote(src, dst, send, recv, peer):
+        return pltpu.make_async_remote_copy(
+            src_ref=src, dst_ref=dst, send_sem=send, recv_sem=recv, device_id=peer, device_id_type=MESH
+        )
+
+    up = remote(edge, edge_low, edge_send.at[0], edge_recv.at[0], {"shot": shot, "depth": lax.rem(depth + 1, nd_dev)})
+    down = remote(edge, edge_high, edge_send.at[1], edge_recv.at[1], {"shot": shot, "depth": lax.rem(depth + nd_dev - 1, nd_dev)})
+
+    @pl.when(depth < nd_dev - 1)
+    def _():
+        up.start()
+
+    @pl.when(depth > 0)
+    def _():
+        down.start()
+
+    @pl.when(depth == 0)
+    def _():
+        edge_low[...] = jnp.zeros_like(edge_low)
+
+    @pl.when(depth == nd_dev - 1)
+    def _():
+        edge_high[...] = jnp.zeros_like(edge_high)
+
+    mark("p03_filter")
+    sums = lax.fori_loop(0, nx // FILTER_ROWS, filter_block, (zero,) * shots)
+
+    mark("p03a_rim")
+    for s in range(shots):
         parts = [packed[g][s] for g in range(groups)]
-        edge[s] = jnp.where(inner, parts[0], pltpu.roll(parts[1], 2, 1))
         backs = [pltpu.roll(part, 4, 1) for part in parts]
         aheads = [pltpu.roll(part, nz - 4, 1) for part in parts]
         for g, part in enumerate(parts):
@@ -165,34 +200,7 @@
             rim_v[s, g] = 6.0 * part - (back + ahead + beside_rows(part) + deep)
             wrap_v[s, g] = jnp.where(place == 1, higher, lower)
 
-    mark("p02b_barrier")
-    pl.semaphore_wait(barrier, len(near) + len(along) + len(corners))
-    mark("p03_halo")
-
-    def remote(src, dst, send, recv, peer):
-        return pltpu.make_async_remote_copy(
-            src_ref=src, dst_ref=dst, send_sem=send, recv_sem=recv, device_id=peer, device_id_type=MESH
-        )
-
-    up = remote(edge, edge_low, edge_send.at[0], edge_recv.at[0], {"shot": shot, "depth": lax.rem(depth + 1, nd_dev)})
-    down = remote(edge, edge_high, edge_send.at[1], edge_recv.at[1], {"shot": shot, "depth": lax.rem(depth + nd_dev - 1, nd_dev)})
-
-    @pl.when(depth < nd_dev - 1)
-    def _():
-        up.start()
-
-    @pl.when(depth > 0)
-    def _():
-        down.start()
-
-    @pl.when(depth == 0)
-    def _():
-        edge_low[...] = jnp.zeros_like(edge_low)
-
-    @pl.when(depth == nd_dev - 1)
-    def _():
-        edge_high[...] = jnp.zeros_like(edge_high)
-
+    mark("p03w_halo")
     @pl.when(depth > 0)
     def _():
         up.wait_recv()
@@ -225,9 +233,13 @@
     next_y = {"shot": after * nz_dev + z, "depth": depth}
     prev_y = {"shot": before * nz_dev + z, "depth": depth}
     next_z, prev_z = along[0], along[-1]
-    order = ring_order(nz_dev)
-    owners = [lax.rem(z + dz, nz_dev) for dz in order]
     opposite = lax.rem(z + nz_dev // 2, nz_dev)
+    def position(owner):
+        return sum(jnp.where(owner == other, k, 0).astype(jnp.int32) for k, other in enumerate(ORDER))
+
+    gap = position(opposite)
+    owners = [jnp.where(i >= gap, ORDER[i + 1], ORDER[i]).astype(jnp.int32) for i in range(nz_dev - 1)]
+    reach = [lax.rem(owner - z + nz_dev, nz_dev) for owner in owners]
 
     def ends_of(packed_side, x):
         return jnp.where(ends, pltpu.roll(packed_side, lax.rem(2 * nz - 2 - 4 * lax.rem(x, group), nz), 1), 0.0)
@@ -300,47 +312,63 @@
         total = blend(0, 0, lambda s: filt[s, x]) - ends_of(mixed[x // group], x)
         if chip and j == chip - 1:
             total = total + blend((ny_dev - 1, 1)[j], 0, lambda s: raw_in[j, s, i])
-        if order[i] == (nz_dev // 2 - 1, nz_dev // 2 + 1)[j]:
-            total = total + blend(0, (nz_dev - 1, 1)[j], lambda s: cross_in[j, s, chip])
-            if chip and j == chip - 1:
+        beyond = jnp.where(reach[i] == (nz_dev // 2 - 1, nz_dev // 2 + 1)[j], 1.0, 0.0).astype(F32)
+        return total + beyond * cross_sum[j, chip]
+
+    for j in range(2):
+        for chip in range(3):
+            total = blend(0, (nz_dev - 1, 1)[j], lambda s: cross_in[j, s, chip])
+            if chip == j + 1:
                 total = total + blend((ny_dev - 1, 1)[j], (nz_dev - 1, 1)[j], lambda s: cross_in[j, s, 3])
-        return total
+            cross_sum[j, chip] = total
 
     moves = []
-    for i in range(len(order)):
+    for i in range(len(owners)):
         for way, peer in enumerate((next_y, prev_y)):
             for j in range(2):
                 sent[way, i, j] = share(i, 1 + way, j)
             copy = remote(sent.at[way, i], got.at[way, i], move_send.at[way, i], move_recv.at[way, i], peer)
+            moves.append(copy)
             copy.start()
-            moves.append(copy)
-    for i in range(len(order)):
+    for i in range(len(owners)):
         for j in range(2):
             image[i, j] = share(i, 0, j)
 
+    mark("p10b_turn")
+
     mark("p11_zsend")
-    finals = []
-    for i, dz in enumerate(order):
+    def final(i):
+        slot = lax.rem(z - owners[i] + nz_dev, nz_dev)
+        peer = {"shot": y * nz_dev + owners[i], "depth": depth}
+        return remote(image.at[i], arrived.at[slot], last_send.at[i], last_recv.at[slot], peer)
+
+    for i, owner in enumerate(owners):
         for way in range(2):
             moves[2 * i + way].wait_recv()
-        value = image[i] + got[0, i] + got[1, i]
-        image[i] = value
-        if dz:
-            copy = remote(image.at[i], arrived.at[i], last_send.at[i], last_recv.at[i], along[dz - 1])
-            copy.start()
-            finals.append(copy)
+        image[i] = image[i] + got[0, i] + got[1, i]
+
+        @pl.when(owner != z)
+        def _(i=i):
+            final(i).start()
+
     mark("p12_zwait")
-    result = value
-    for i, copy in enumerate(finals):
-        copy.wait_recv()
-        result = result + arrived[i]
+    result = image[position(z) - jnp.where(position(z) > gap, 1, 0).astype(jnp.int32)]
+    for dz in sorted(range(1, nz_dev), key=lambda d: min(d, nz_dev - d)):
+        if 2 * dz != nz_dev:
+            pltpu.make_async_copy(arrived.at[dz], arrived.at[dz], last_recv.at[dz]).wait()
+            result = result + arrived[dz]
     out[...] = result
 
     mark("p13_tail")
-    for copy in finals:
+    for i, owner in enumerate(owners):
+
+        @pl.when(owner != z)
+        def _(i=i):
+            final(i).wait_send()
+
+    for copy in raws + moves:
         copy.wait_send()
-    for copy in moves + raws:
-        copy.wait_send()
+
     pltpu.make_async_copy(others, others, small_send.at[0]).wait()
     pltpu.make_async_copy(rest, rest, small_send.at[1]).wait()
 
@@ -366,7 +394,7 @@
         assert per_z == 2 and nz == 128 and nx == 64
         dma = pltpu.SemaphoreType.DMA
         field = (ny, nz)
-        chunks = len(ring_order(nz_dev))
+        chunks = nz_dev - 1
         return pl.pallas_call(
             functools.partial(kernel, ny_dev, nz_dev, nd_dev),
             out_shape=jax.ShapeDtypeStruct((per_z, ny, nz), F32),
@@ -376,7 +404,7 @@
                 pltpu.SMEM((shots, 4), jnp.int32),
                 pltpu.VMEM((shots, nx, *field), F32),
                 pltpu.VMEM((shots, nx, *field), F32),
-                pltpu.VMEM((shots, nx + 2, *field), F32),
+                pltpu.VMEM((shots, nx + 2, ny + 2 * PAD, nz), F32),
                 pltpu.VMEM((shots, nx, *field), F32),
                 pltpu.VMEM((shots, *field), F32),
                 pltpu.VMEM((shots, *field), F32),
@@ -391,14 +419,15 @@
                 pltpu.VMEM((2, shots, chunks, *field), F32),
                 pltpu.VMEM((2, shots, 4, *field), F32),
                 pltpu.VMEM((2, shots, 4, *field), F32),
+                pltpu.VMEM((2, 3, *field), F32),
                 pltpu.VMEM((2, chunks, per_z, *field), F32),
                 pltpu.VMEM((2, chunks, per_z, *field), F32),
                 pltpu.VMEM((chunks, per_z, *field), F32),
-                pltpu.VMEM((chunks - 1, per_z, *field), F32),
+                pltpu.VMEM((nz_dev, per_z, *field), F32),
                 dma, dma((shots, PIECES, 2)),
                 dma((2,)), dma((2,)), dma((2,)), dma((2,)),
                 dma((3, 2)), dma((3, 2)), dma((2, chunks)), dma((2, chunks)),
-                dma((chunks - 1,)), dma((chunks - 1,)),
+                dma((chunks,)), dma((nz_dev,)),
             ],
             compiler_params=pltpu.CompilerParams(
                 collective_id=0, has_side_effects=True, vmem_limit_bytes=32 << 20

time: 32.8 us -> 31.9 us (0.973)
  the two profiles are of different devices: /device:TPU:8 before, /device:TPU:4 now
where the time goes in v4:
time: 31.9 us; the launch traced here: 31.3 us
  Pallas kernels  30.7 us (96%)
  local copies, waits for them, and re-layouts  0.62 us (2%)
    pallas_call x1, Pallas kernels, on_device(): pl.pallas_call(functools.partial(kernel, ny_dev, nz_dev, nd_dev), out_sha...  30.7 us

profile of v4, /device:TPU:4, one launch (start us, length us, event | category | flops | bytes accessed | tf_op | source)
XLA Modules:
  0.0 31.3 jit_solution(3378396193870443232)
XLA Ops:
  0.0 30.7 %shard_map.37 = f32[2,32,128]{2,1,0:T(8,128)S(1)} custom-call(s32[2,4]{1,0:T(2,128)} %box_hbm.1, f32[2,64,32,128]{3,2,1,0:T(8,128)} %corr.1, f32[2,64,32,128]{3,2,1,0:T(8,128)} %illum.1), custom_call_target="tpu_custom_call" | custom-call | tf_op jit(solution)/shard_map/pallas_call | solution.py:398
  30.7 0.6 %copy.5 = f32[2,32,128]{2,1,0:T(8,128)} copy(f32[2,32,128]{2,1,0:T(8,128)S(1)} %shard_map.37) | data formatting | bytes 65536

commit v5 on v4

--- a/solution.py
+++ b/solution.py
@@ -12,7 +12,7 @@
 NORM_ROWS = 16
 FILTER_ROWS = 16
 PAD = 8
-ORDER = (0, 1, 2, 3, 7, 6, 5, 4)
+REACH = (-3, 3, 1, -1, 0)
 F32 = jnp.float32
 MESH = pl.DeviceIdType.MESH
 
@@ -34,7 +34,7 @@
     ny_dev, nz_dev, nd_dev,
     box_hbm, corr, illum, out,
     box, corr_v, illum_v, norm, filt, edge, edge_low, edge_high, rim_v, wrap_v, side_v, mixed,
-    energy, peaks, raw_out, raw_in, cross_out, cross_in, cross_sum, sent, got, image, arrived,
+    energy, peaks, raw_out, raw_in, cross_out, cross_in, beside_out, beside_in, corner_out, corner_in, direct, sent, got, image, arrived,
     box_sem, load_sem, edge_send, edge_recv, small_send, small_recv,
     raw_send, raw_recv, move_send, move_recv, last_send, last_recv,
 ):
@@ -75,10 +75,13 @@
     after, before, across = (lax.rem(y + d, ny_dev) for d in (1, ny_dev - 1, ny_dev // 2))
     corners = [
         {"shot": side * nz_dev + lax.rem(z + d, nz_dev), "depth": depth}
-        for side, d in ((after, 1), (before, nz_dev - 1))
+        for d in (1, nz_dev - 1)
+        for side in (after, before)
     ]
     barrier = pltpu.get_barrier_semaphore()
-    for peer in near + along + corners:
+    core = lax.rem(depth, 2)
+    cross_core = [{"shot": peer["shot"], "depth": depth + 1 - 2 * core} for peer in along]
+    for peer in near + along + cross_core + corners:
         pl.semaphore_signal(barrier, inc=1, device_id=peer, device_id_type=MESH)
     for piece in loads[1:]:
         for copy in piece:
@@ -153,11 +156,13 @@
 
     mark("p02_pack")
     inner = (place == 1) | (place == 2)
-    for s in range(shots):
-        edge[s] = jnp.where(inner, packed[0][s], pltpu.roll(packed[1][s], 2, 1))
+    rims = [jnp.where(inner, packed[0][s], pltpu.roll(packed[1][s], 2, 1)) for s in range(shots)]
+    odd = lax.rem(lane, 2) == 1
+    edge[0] = jnp.where(odd, rims[0], pltpu.roll(rims[1], 1, 1))
+    edge[1] = jnp.where(odd, pltpu.roll(rims[1], nz - 1, 1), rims[0])
 
     mark("p02b_barrier")
-    pl.semaphore_wait(barrier, len(near) + len(along) + len(corners))
+    pl.semaphore_wait(barrier, len(near) + len(along) + len(cross_core) + len(corners))
     mark("p03_halo")
 
     def remote(src, dst, send, recv, peer):
@@ -165,8 +170,8 @@
             src_ref=src, dst_ref=dst, send_sem=send, recv_sem=recv, device_id=peer, device_id_type=MESH
         )
 
-    up = remote(edge, edge_low, edge_send.at[0], edge_recv.at[0], {"shot": shot, "depth": lax.rem(depth + 1, nd_dev)})
-    down = remote(edge, edge_high, edge_send.at[1], edge_recv.at[1], {"shot": shot, "depth": lax.rem(depth + nd_dev - 1, nd_dev)})
+    up = remote(edge.at[0], edge_low, edge_send.at[0], edge_recv.at[0], {"shot": shot, "depth": lax.rem(depth + 1, nd_dev)})
+    down = remote(edge.at[1], edge_high, edge_send.at[1], edge_recv.at[1], {"shot": shot, "depth": lax.rem(depth + nd_dev - 1, nd_dev)})
 
     @pl.when(depth < nd_dev - 1)
     def _():
@@ -212,20 +217,25 @@
     mark("p04_energy")
     for s in range(shots):
         total = jnp.where(ends, 0.0, sums[s])
-        high, low = edge_high[s], edge_low[s]
+        high, low = edge_high[...], edge_low[...]
         for g in range(groups):
             side = jnp.where(
                 place == 1,
-                pltpu.roll(high, (nz - 1 - 2 * g) % nz, 1),
-                pltpu.roll(low, (nz + 1 - 2 * g) % nz, 1),
+                pltpu.roll(high, (nz - 1 - 2 * g + s) % nz, 1),
+                pltpu.roll(low, (nz + 1 - 2 * g - s) % nz, 1),
             )
             side_v[s, g] = side - wrap_v[s, g]
             rim = rim_v[s, g] - side
             total = total + jnp.where(inner, rim * rim, 0.0)
         energy[0, s : s + 1] = jnp.sum(total, axis=0, keepdims=True)
 
-    for i, peer in enumerate(near):
+    def span(i):
         dy, dd = (i + 1) // nd_dev, (i + 1) % nd_dev
+        return min(dy, ny_dev - dy) + min(dd, nd_dev - dd) / 2
+
+    for i in sorted(range(len(near)), key=span, reverse=True):
+        dy, dd = (i + 1) // nd_dev, (i + 1) % nd_dev
+        peer = near[i]
         slot = ((ny_dev - dy) % ny_dev) * nd_dev + (nd_dev - dd) % nd_dev
         remote(energy.at[0], energy.at[slot], small_send.at[0], small_recv.at[0], peer).start()
 
@@ -233,13 +243,9 @@
     next_y = {"shot": after * nz_dev + z, "depth": depth}
     prev_y = {"shot": before * nz_dev + z, "depth": depth}
     next_z, prev_z = along[0], along[-1]
+    owners = [lax.rem(z + nz_dev + dz, nz_dev) for dz in REACH]
     opposite = lax.rem(z + nz_dev // 2, nz_dev)
-    def position(owner):
-        return sum(jnp.where(owner == other, k, 0).astype(jnp.int32) for k, other in enumerate(ORDER))
-
-    gap = position(opposite)
-    owners = [jnp.where(i >= gap, ORDER[i + 1], ORDER[i]).astype(jnp.int32) for i in range(nz_dev - 1)]
-    reach = [lax.rem(owner - z + nz_dev, nz_dev) for owner in owners]
+    seconds = [lax.rem(z + 2, nz_dev), lax.rem(z + nz_dev - 2, nz_dev)]
 
     def ends_of(packed_side, x):
         return jnp.where(ends, pltpu.roll(packed_side, lax.rem(2 * nz - 2 - 4 * lax.rem(x, group), nz), 1), 0.0)
@@ -247,31 +253,40 @@
     def raw(s, x):
         return filt[s, x] - ends_of(side_v[s, x // group], x)
 
-    chips = (y, after, before, across)
+    chips = (y, after, before)
+    raws = []
+
+    def push(out_ref, in_ref, index, peer):
+        copy = remote(out_ref, in_ref, raw_send.at[index], raw_recv.at[index], peer)
+        copy.start()
+        raws.append(copy)
+
     for way in range(2):
         for s in range(shots):
             for i, chip in enumerate(chips):
                 cross_out[way, s, i] = raw(s, chip * per_y + 2 * opposite + way)
-    raws = []
-    for way in range(2):
-        straight, corner = pl.ds(0, 3), pl.ds(3, 1)
-        raws.append(remote(
-            cross_out.at[way, :, straight], cross_in.at[way, :, straight],
-            raw_send.at[0, way], raw_recv.at[0, way], (next_z, prev_z)[way],
-        ))
-        raws.append(remote(
-            cross_out.at[way, :, corner], cross_in.at[way, :, corner],
-            raw_send.at[1, way], raw_recv.at[1, way], corners[way],
-        ))
-    for copy in raws:
-        copy.start()
+    for way in range(2):
+        push(cross_out.at[way], cross_in.at[way], way, (next_z, prev_z)[way])
     for way in range(2):
         for s in range(shots):
             for i, owner in enumerate(owners):
                 raw_out[way, s, i] = raw(s, across * per_y + 2 * owner + way)
-        copy = remote(raw_out.at[way], raw_in.at[way], raw_send.at[2, way], raw_recv.at[2, way], (next_y, prev_y)[way])
-        copy.start()
-        raws.append(copy)
+    for way in range(2):
+        push(raw_out.at[way], raw_in.at[way], 2 + way, (next_y, prev_y)[way])
+    for way in range(2):
+        for j in range(2):
+            for s in range(shots):
+                for i, chip in enumerate(chips[1:]):
+                    beside_out[way, j, s, i] = raw(s, chip * per_y + 2 * seconds[way] + j)
+    for way in range(2):
+        for j in range(2):
+            for s in range(shots):
+                corner_out[2 * way + j, 0, s] = raw(s, across * per_y + 2 * seconds[way] + j)
+                if j == way:
+                    corner_out[2 * way + j, 1, s] = raw(s, across * per_y + 2 * opposite + j)
+    for k in range(4):
+        part = pl.ds(0, 2 if k in (0, 3) else 1)
+        push(corner_out.at[k, part], corner_in.at[k, part], 6 + k, corners[k])
 
     mark("p06_wait_energy")
     others = energy.at[pl.ds(1, len(near))]
@@ -284,8 +299,15 @@
         means.append(jnp.broadcast_to(jnp.sum(both, axis=1, keepdims=True) / cells, (shots, nz)))
     for dy in range(ny_dev):
         peaks[0, dy * shots : (dy + 1) * shots] = means[dy]
-    for i, peer in enumerate(along):
-        remote(peaks.at[0], peaks.at[nz_dev - 1 - i], small_send.at[1], small_recv.at[1], peer).start()
+
+    @pl.when(core == 1)
+    def _():
+        for peers in (cross_core, along):
+            for i, peer in enumerate(peers):
+                remote(peaks.at[0], peaks.at[nz_dev - 1 - i], small_send.at[1], small_recv.at[1], peer).start()
+
+    for way in range(2):
+        push(beside_out.at[way], beside_in.at[way], 4 + way, (next_z, prev_z)[way])
     rest = peaks.at[pl.ds(1, len(along))]
     mark("p08_wait_peak")
     pltpu.make_async_copy(rest, rest, small_recv.at[1]).wait()
@@ -304,26 +326,46 @@
         mixed[g] = blend(0, 0, lambda s: side_v[s, g])
 
     mark("p10_ysend")
-    for copy in raws:
+    for copy in raws[:8]:
         copy.wait_recv()
+
+    low, high = nz_dev - 1, 1
+    behind, ahead = ny_dev - 1, 1
 
     def share(i, chip, j):
         x = chips[chip] * per_y + 2 * owners[i] + j
         total = blend(0, 0, lambda s: filt[s, x]) - ends_of(mixed[x // group], x)
-        if chip and j == chip - 1:
-            total = total + blend((ny_dev - 1, 1)[j], 0, lambda s: raw_in[j, s, i])
-        beyond = jnp.where(reach[i] == (nz_dev // 2 - 1, nz_dev // 2 + 1)[j], 1.0, 0.0).astype(F32)
-        return total + beyond * cross_sum[j, chip]
-
-    for j in range(2):
-        for chip in range(3):
-            total = blend(0, (nz_dev - 1, 1)[j], lambda s: cross_in[j, s, chip])
-            if chip == j + 1:
-                total = total + blend((ny_dev - 1, 1)[j], (nz_dev - 1, 1)[j], lambda s: cross_in[j, s, 3])
-            cross_sum[j, chip] = total
+        onward = chip and j == chip - 1
+        side = (behind, ahead)[j]
+        if onward:
+            total = total + blend(side, 0, lambda s: raw_in[j, s, i])
+        if REACH[i] == (3, -3)[j]:
+            total = total + blend(0, (low, high)[j], lambda s: cross_in[j, s, chip])
+            if onward:
+                total = total + blend(side, (low, high)[j], lambda s: corner_in[3 * j, 1, s])
+        if REACH[i] in (1, -1):
+            way = (1, -1).index(REACH[i])
+            if chip:
+                total = total + blend(0, (low, high)[way], lambda s: beside_in[way, j, s, chip - 1])
+            if onward:
+                total = total + blend(side, (low, high)[way], lambda s: corner_in[2 * way + j, 0, s])
+        return total
+
+    finals = []
+    for way in range(2):
+        for j in range(2):
+            x = y * per_y + 2 * seconds[way] + j
+            direct[way, j] = blend(0, 0, lambda s: filt[s, x]) - ends_of(mixed[x // group], x)
+        slot = len(REACH) + way
+        copy = remote(direct.at[way], arrived.at[slot], last_send.at[slot], last_recv.at[slot], along[(1, nz_dev - 3)[way]])
+        copy.start()
+        finals.append((copy, slot))
 
     moves = []
     for i in range(len(owners)):
+        if i == min(REACH.index(1), REACH.index(-1)):
+            for copy in raws[8:]:
+                copy.wait_recv()
         for way, peer in enumerate((next_y, prev_y)):
             for j in range(2):
                 sent[way, i, j] = share(i, 1 + way, j)
@@ -337,40 +379,36 @@
     mark("p10b_turn")
 
     mark("p11_zsend")
-    def final(i):
-        slot = lax.rem(z - owners[i] + nz_dev, nz_dev)
-        peer = {"shot": y * nz_dev + owners[i], "depth": depth}
-        return remote(image.at[i], arrived.at[slot], last_send.at[i], last_recv.at[slot], peer)
-
-    for i, owner in enumerate(owners):
+    for i, dz in enumerate(REACH):
         for way in range(2):
             moves[2 * i + way].wait_recv()
-        image[i] = image[i] + got[0, i] + got[1, i]
-
-        @pl.when(owner != z)
-        def _(i=i):
-            final(i).start()
-
+        value = image[i] + got[0, i] + got[1, i]
+        image[i] = value
+        if dz:
+            peer = along[(dz - 1) % nz_dev]
+            copy = remote(image.at[i], arrived.at[i], last_send.at[i], last_recv.at[i], peer)
+            copy.start()
+            finals.append((copy, i))
     mark("p12_zwait")
-    result = image[position(z) - jnp.where(position(z) > gap, 1, 0).astype(jnp.int32)]
-    for dz in sorted(range(1, nz_dev), key=lambda d: min(d, nz_dev - d)):
-        if 2 * dz != nz_dev:
-            pltpu.make_async_copy(arrived.at[dz], arrived.at[dz], last_recv.at[dz]).wait()
-            result = result + arrived[dz]
+    result = image[REACH.index(0)]
+    for copy, slot in finals:
+        copy.wait_recv()
+        result = result + arrived[slot]
     out[...] = result
 
     mark("p13_tail")
-    for i, owner in enumerate(owners):
-
-        @pl.when(owner != z)
-        def _(i=i):
-            final(i).wait_send()
-
+    for copy, _ in finals:
+        copy.wait_send()
     for copy in raws + moves:
         copy.wait_send()
 
     pltpu.make_async_copy(others, others, small_send.at[0]).wait()
-    pltpu.make_async_copy(rest, rest, small_send.at[1]).wait()
+
+    @pl.when(core == 1)
+    def _():
+        pltpu.make_async_copy(rest, rest, small_send.at[1]).wait()
+        pltpu.make_async_copy(rest, rest, small_send.at[1]).wait()
+
 
     @pl.when(depth < nd_dev - 1)
     def _():
@@ -391,10 +429,10 @@
     def on_device(correlation, illumination, aperture):
         shots, nx, ny, nz = correlation.shape
         per_z = nx // ny_dev // nz_dev
-        assert per_z == 2 and nz == 128 and nx == 64
+        assert per_z == 2 and nz == 128 and nx == 64 and nz_dev == 8
         dma = pltpu.SemaphoreType.DMA
         field = (ny, nz)
-        chunks = nz_dev - 1
+        chunks = len(REACH)
         return pl.pallas_call(
             functools.partial(kernel, ny_dev, nz_dev, nd_dev),
             out_shape=jax.ShapeDtypeStruct((per_z, ny, nz), F32),
@@ -407,8 +445,8 @@
                 pltpu.VMEM((shots, nx + 2, ny + 2 * PAD, nz), F32),
                 pltpu.VMEM((shots, nx, *field), F32),
                 pltpu.VMEM((shots, *field), F32),
-                pltpu.VMEM((shots, *field), F32),
-                pltpu.VMEM((shots, *field), F32),
+                pltpu.VMEM(field, F32),
+                pltpu.VMEM(field, F32),
                 pltpu.VMEM((shots, 2, *field), F32),
                 pltpu.VMEM((shots, 2, *field), F32),
                 pltpu.VMEM((shots, 2, *field), F32),
@@ -417,17 +455,21 @@
                 pltpu.VMEM((nz_dev, ny_dev * shots, nz), F32),
                 pltpu.VMEM((2, shots, chunks, *field), F32),
                 pltpu.VMEM((2, shots, chunks, *field), F32),
-                pltpu.VMEM((2, shots, 4, *field), F32),
-                pltpu.VMEM((2, shots, 4, *field), F32),
-                pltpu.VMEM((2, 3, *field), F32),
+                pltpu.VMEM((2, shots, 3, *field), F32),
+                pltpu.VMEM((2, shots, 3, *field), F32),
+                pltpu.VMEM((2, 2, shots, 2, *field), F32),
+                pltpu.VMEM((2, 2, shots, 2, *field), F32),
+                pltpu.VMEM((4, 2, shots, *field), F32),
+                pltpu.VMEM((4, 2, shots, *field), F32),
+                pltpu.VMEM((2, per_z, *field), F32),
                 pltpu.VMEM((2, chunks, per_z, *field), F32),
                 pltpu.VMEM((2, chunks, per_z, *field), F32),
                 pltpu.VMEM((chunks, per_z, *field), F32),
-                pltpu.VMEM((nz_dev, per_z, *field), F32),
+                pltpu.VMEM((chunks + 2, per_z, *field), F32),
                 dma, dma((shots, PIECES, 2)),
                 dma((2,)), dma((2,)), dma((2,)), dma((2,)),
-                dma((3, 2)), dma((3, 2)), dma((2, chunks)), dma((2, chunks)),
-                dma((chunks,)), dma((nz_dev,)),
+                dma((10,)), dma((10,)), dma((2, chunks)), dma((2, chunks)),
+                dma((chunks + 2,)), dma((chunks + 2,)),
             ],
             compiler_params=pltpu.CompilerParams(
                 collective_id=0, has_side_effects=True, vmem_limit_bytes=32 << 20

time: 31.9 us -> 31.7 us (level); the launches traced: 31.3 us -> 31.6 us
    pallas_call x1, Pallas kernels: 30.7 us -> 31 us  [on_device(): pl.pallas_call(functools.partial(kernel, ny_dev, nz_dev, nd_dev), out_sha...]
where the time goes in v5:
time: 31.7 us; the launch traced here: 31.6 us
  Pallas kernels  31 us (98%)
  local copies, waits for them, and re-layouts  0.62 us (2%)
    pallas_call x1, Pallas kernels, on_device(): pl.pallas_call(functools.partial(kernel, ny_dev, nz_dev, nd_dev), out_sha...  31 us

profile of v5, /device:TPU:4, one launch (start us, length us, event | category | flops | bytes accessed | tf_op | source)
XLA Modules:
  0.0 31.6 jit_solution(5906236194729204397)
XLA Ops:
  0.0 31.0 %shard_map.37 = f32[2,32,128]{2,1,0:T(8,128)S(1)} custom-call(s32[2,4]{1,0:T(2,128)} %box_hbm.1, f32[2,64,32,128]{3,2,1,0:T(8,128)} %corr.1, f32[2,64,32,128]{3,2,1,0:T(8,128)} %illum.1), custom_call_target="tpu_custom_call" | custom-call | tf_op jit(solution)/shard_map/pallas_call | solution.py:436
  31.0 0.6 %copy.5 = f32[2,32,128]{2,1,0:T(8,128)} copy(f32[2,32,128]{2,1,0:T(8,128)S(1)} %shard_map.37) | data formatting | bytes 65536

commit v6 on v5

--- a/solution.py
+++ b/solution.py
@@ -13,6 +13,7 @@
 FILTER_ROWS = 16
 PAD = 8
 REACH = (-3, 3, 1, -1, 0)
+EARLY = ((0, 3), (0, -3))
 F32 = jnp.float32
 MESH = pl.DeviceIdType.MESH
 
@@ -34,7 +35,7 @@
     ny_dev, nz_dev, nd_dev,
     box_hbm, corr, illum, out,
     box, corr_v, illum_v, norm, filt, edge, edge_low, edge_high, rim_v, wrap_v, side_v, mixed,
-    energy, peaks, raw_out, raw_in, cross_out, cross_in, beside_out, beside_in, corner_out, corner_in, direct, sent, got, image, arrived,
+    energy, peaks, raw_out, raw_in, cross_out, cross_in, beside_out, beside_in, corner_out, corner_in, early_out, early_in, direct, sent, got, image, arrived,
     box_sem, load_sem, edge_send, edge_recv, small_send, small_recv,
     raw_send, raw_recv, move_send, move_recv, last_send, last_recv,
 ):
@@ -81,7 +82,15 @@
     barrier = pltpu.get_barrier_semaphore()
     core = lax.rem(depth, 2)
     cross_core = [{"shot": peer["shot"], "depth": depth + 1 - 2 * core} for peer in along]
-    for peer in near + along + cross_core + corners:
+
+    def hops(count, d):
+        return min(d, count - d)
+
+    far = [hops(ny_dev, (i + 1) // nd_dev) + hops(nd_dev, (i + 1) % nd_dev) / 2 for i in range(len(near))]
+    far += [hops(nz_dev, i + 1) for i in range(len(along))] * 2 + [2] * len(corners)
+    greeted = near + along + cross_core + corners
+    for i in sorted(range(len(greeted)), key=lambda i: -far[i]):
+        peer = greeted[i]
         pl.semaphore_signal(barrier, inc=1, device_id=peer, device_id_type=MESH)
     for piece in loads[1:]:
         for copy in piece:
@@ -287,6 +296,14 @@
     for k in range(4):
         part = pl.ds(0, 2 if k in (0, 3) else 1)
         push(corner_out.at[k, part], corner_in.at[k, part], 6 + k, corners[k])
+    earlies = []
+    for way in range(2):
+        for n, dz in enumerate(EARLY[way]):
+            for s in range(shots):
+                early_out[way, n, s] = raw(s, chips[1 + way] * per_y + 2 * owners[REACH.index(dz)] + 1 - way)
+        copy = remote(early_out.at[way], early_in.at[way], raw_send.at[10 + way], raw_recv.at[10 + way], (next_y, prev_y)[way])
+        copy.start()
+        earlies.append(copy)
 
     mark("p06_wait_energy")
     others = energy.at[pl.ds(1, len(near))]
@@ -339,6 +356,9 @@
         side = (behind, ahead)[j]
         if onward:
             total = total + blend(side, 0, lambda s: raw_in[j, s, i])
+        if not chip and REACH[i] in EARLY[1 - j]:
+            n = EARLY[1 - j].index(REACH[i])
+            total = total + blend((behind, ahead)[1 - j], 0, lambda s: early_in[1 - j, n, s])
         if REACH[i] == (3, -3)[j]:
             total = total + blend(0, (low, high)[j], lambda s: cross_in[j, s, chip])
             if onward:
@@ -351,27 +371,31 @@
                 total = total + blend(side, (low, high)[way], lambda s: corner_in[2 * way + j, 0, s])
         return total
 
-    finals = []
-    for way in range(2):
-        for j in range(2):
-            x = y * per_y + 2 * seconds[way] + j
-            direct[way, j] = blend(0, 0, lambda s: filt[s, x]) - ends_of(mixed[x // group], x)
-        slot = len(REACH) + way
-        copy = remote(direct.at[way], arrived.at[slot], last_send.at[slot], last_recv.at[slot], along[(1, nz_dev - 3)[way]])
-        copy.start()
-        finals.append((copy, slot))
-
-    moves = []
+    def rows_of(way, i):
+        return (way,) if REACH[i] in EARLY[way] else (0, 1)
+
+    moves, finals = [], []
     for i in range(len(owners)):
-        if i == min(REACH.index(1), REACH.index(-1)):
+        if i == 2:
+            for way in range(2):
+                for j in range(2):
+                    x = y * per_y + 2 * seconds[way] + j
+                    direct[way, j] = blend(0, 0, lambda s: filt[s, x]) - ends_of(mixed[x // group], x)
+                slot = len(REACH) + way
+                copy = remote(direct.at[way], arrived.at[slot], last_send.at[slot], last_recv.at[slot], along[(1, nz_dev - 3)[way]])
+                copy.start()
+                finals.append((copy, slot))
             for copy in raws[8:]:
                 copy.wait_recv()
         for way, peer in enumerate((next_y, prev_y)):
-            for j in range(2):
+            for j in rows_of(way, i):
                 sent[way, i, j] = share(i, 1 + way, j)
-            copy = remote(sent.at[way, i], got.at[way, i], move_send.at[way, i], move_recv.at[way, i], peer)
+            part = pl.ds(rows_of(way, i)[0], len(rows_of(way, i)))
+            copy = remote(sent.at[way, i, part], got.at[way, i, part], move_send.at[way, i], move_recv.at[way, i], peer)
             moves.append(copy)
             copy.start()
+    for copy in earlies:
+        copy.wait_recv()
     for i in range(len(owners)):
         for j in range(2):
             image[i, j] = share(i, 0, j)
@@ -382,8 +406,12 @@
     for i, dz in enumerate(REACH):
         for way in range(2):
             moves[2 * i + way].wait_recv()
-        value = image[i] + got[0, i] + got[1, i]
-        image[i] = value
+        for j in range(2):
+            value = image[i, j]
+            for way in range(2):
+                if j in rows_of(way, i):
+                    value = value + got[way, i, j]
+            image[i, j] = value
         if dz:
             peer = along[(dz - 1) % nz_dev]
             copy = remote(image.at[i], arrived.at[i], last_send.at[i], last_recv.at[i], peer)
@@ -399,7 +427,7 @@
     mark("p13_tail")
     for copy, _ in finals:
         copy.wait_send()
-    for copy in raws + moves:
+    for copy in raws + earlies + moves:
         copy.wait_send()
 
     pltpu.make_async_copy(others, others, small_send.at[0]).wait()
@@ -461,6 +489,8 @@
                 pltpu.VMEM((2, 2, shots, 2, *field), F32),
                 pltpu.VMEM((4, 2, shots, *field), F32),
                 pltpu.VMEM((4, 2, shots, *field), F32),
+                pltpu.VMEM((2, 2, shots, *field), F32),
+                pltpu.VMEM((2, 2, shots, *field), F32),
                 pltpu.VMEM((2, per_z, *field), F32),
                 pltpu.VMEM((2, chunks, per_z, *field), F32),
                 pltpu.VMEM((2, chunks, per_z, *field), F32),
@@ -468,7 +498,7 @@
                 pltpu.VMEM((chunks + 2, per_z, *field), F32),
                 dma, dma((shots, PIECES, 2)),
                 dma((2,)), dma((2,)), dma((2,)), dma((2,)),
-                dma((10,)), dma((10,)), dma((2, chunks)), dma((2, chunks)),
+                dma((12,)), dma((12,)), dma((2, chunks)), dma((2, chunks)),
                 dma((chunks + 2,)), dma((chunks + 2,)),
             ],
             compiler_params=pltpu.CompilerParams(

time: 31.7 us -> 31.2 us (0.984)
  Pallas kernels: 31 us -> 30.2 us
    pallas_call x1, Pallas kernels: 31 us -> 30.2 us  [on_device(): pl.pallas_call(functools.partial(kernel, ny_dev, nz_dev, nd_dev), out_sha...]
where the time goes in v6:
time: 31.2 us; the launch traced here: 30.9 us
  Pallas kernels  30.2 us (97%)
  local copies, waits for them, and re-layouts  0.62 us (2%)
    pallas_call x1, Pallas kernels, on_device(): pl.pallas_call(functools.partial(kernel, ny_dev, nz_dev, nd_dev), out_sha...  30.2 us

profile of v6, /device:TPU:4, one launch (start us, length us, event | category | flops | bytes accessed | tf_op | source)
XLA Modules:
  0.0 30.9 jit_solution(16149640758443293536)
XLA Ops:
  0.0 30.2 %shard_map.37 = f32[2,32,128]{2,1,0:T(8,128)S(1)} custom-call(s32[2,4]{1,0:T(2,128)} %box_hbm.1, f32[2,64,32,128]{3,2,1,0:T(8,128)} %corr.1, f32[2,64,32,128]{3,2,1,0:T(8,128)} %illum.1), custom_call_target="tpu_custom_call" | custom-call | tf_op jit(solution)/shard_map/pallas_call | solution.py:464
  30.2 0.6 %copy.5 = f32[2,32,128]{2,1,0:T(8,128)} copy(f32[2,32,128]{2,1,0:T(8,128)S(1)} %shard_map.37) | data formatting | bytes 65536

commit v7 on v6

--- a/solution.py
+++ b/solution.py
@@ -12,7 +12,7 @@
 NORM_ROWS = 16
 FILTER_ROWS = 16
 PAD = 8
-REACH = (-3, 3, 1, -1, 0)
+REACH = (3, -3, 1, -1, 0)
 EARLY = ((0, 3), (0, -3))
 F32 = jnp.float32
 MESH = pl.DeviceIdType.MESH
@@ -246,7 +246,8 @@
         dy, dd = (i + 1) // nd_dev, (i + 1) % nd_dev
         peer = near[i]
         slot = ((ny_dev - dy) % ny_dev) * nd_dev + (nd_dev - dd) % nd_dev
-        remote(energy.at[0], energy.at[slot], small_send.at[0], small_recv.at[0], peer).start()
+        copy = remote(energy.at[0], energy.at[slot], small_send.at[0], small_recv.at[0], peer)
+        pl.when(core == 1 - dd % 2)(copy.start)
 
     mark("p05_raw")
     next_y = {"shot": after * nz_dev + z, "depth": depth}
@@ -307,21 +308,26 @@
 
     mark("p06_wait_energy")
     others = energy.at[pl.ds(1, len(near))]
-    pltpu.make_async_copy(others, others, small_recv.at[0]).wait()
-    mark("p07_means")
     cells = nx * ny * nz * nd_dev
-    means = []
-    for dy in range(ny_dev):
-        both = jnp.sum(energy[dy * nd_dev : (dy + 1) * nd_dev], axis=0)
-        means.append(jnp.broadcast_to(jnp.sum(both, axis=1, keepdims=True) / cells, (shots, nz)))
-    for dy in range(ny_dev):
-        peaks[0, dy * shots : (dy + 1) * shots] = means[dy]
+
+    def told(src, dst, peer, recv):
+        return remote(peaks.at[src], peaks.at[dst], small_send.at[1], small_recv.at[recv], peer)
 
     @pl.when(core == 1)
     def _():
+        pltpu.make_async_copy(others, others, small_recv.at[0]).wait()
+        for dy in range(ny_dev):
+            both = jnp.sum(energy[dy * nd_dev : (dy + 1) * nd_dev], axis=0)
+            mean = jnp.sum(both, axis=1, keepdims=True) / cells
+            peaks[0, dy * shots : (dy + 1) * shots] = jnp.broadcast_to(mean, (shots, nz))
         for peers in (cross_core, along):
             for i, peer in enumerate(peers):
-                remote(peaks.at[0], peaks.at[nz_dev - 1 - i], small_send.at[1], small_recv.at[1], peer).start()
+                told(0, nz_dev - 1 - i, peer, 1).start()
+        told(0, 0, {"shot": shot, "depth": depth - 1}, 2).start()
+
+    @pl.when(core == 0)
+    def _():
+        pltpu.make_async_copy(peaks.at[0], peaks.at[0], small_recv.at[2]).wait()
 
     for way in range(2):
         push(beside_out.at[way], beside_in.at[way], 4 + way, (next_z, prev_z)[way])
@@ -430,12 +436,14 @@
     for copy in raws + earlies + moves:
         copy.wait_send()
 
-    pltpu.make_async_copy(others, others, small_send.at[0]).wait()
+    for k in range(2):
+        part = energy.at[pl.ds(1, len(near) // 2 + 1 - k)]
+        pl.when(core == k)(pltpu.make_async_copy(part, part, small_send.at[0]).wait)
 
     @pl.when(core == 1)
     def _():
         pltpu.make_async_copy(rest, rest, small_send.at[1]).wait()
-        pltpu.make_async_copy(rest, rest, small_send.at[1]).wait()
+        pltpu.make_async_copy(peaks, peaks, small_send.at[1]).wait()
 
 
     @pl.when(depth < nd_dev - 1)
@@ -497,7 +505,7 @@
                 pltpu.VMEM((chunks, per_z, *field), F32),
                 pltpu.VMEM((chunks + 2, per_z, *field), F32),
                 dma, dma((shots, PIECES, 2)),
-                dma((2,)), dma((2,)), dma((2,)), dma((2,)),
+                dma((2,)), dma((2,)), dma((2,)), dma((3,)),
                 dma((12,)), dma((12,)), dma((2, chunks)), dma((2, chunks)),
                 dma((chunks + 2,)), dma((chunks + 2,)),
             ],

time: 31.2 us -> 30.7 us (0.984)
  no operation moved by 1% of the time
where the time goes in v7:
time: 30.7 us; the launch traced here: 30.6 us
  Pallas kernels  30 us (98%)
  local copies, waits for them, and re-layouts  0.62 us (2%)
    pallas_call x1, Pallas kernels, on_device(): pl.pallas_call(functools.partial(kernel, ny_dev, nz_dev, nd_dev), out_sha...  30 us
    unnamed x1, local copies, waits for them, and re-layouts  0.62 us

profile of v7, /device:TPU:4, one launch (start us, length us, event | category | flops | bytes accessed | tf_op | source)
XLA Modules:
  0.0 30.6 jit_solution(17301293568501138207)
XLA Ops:
  0.0 30.0 %shard_map.37 = f32[2,32,128]{2,1,0:T(8,128)S(1)} custom-call(s32[2,4]{1,0:T(2,128)} %box_hbm.1, f32[2,64,32,128]{3,2,1,0:T(8,128)} %corr.1, f32[2,64,32,128]{3,2,1,0:T(8,128)} %illum.1), custom_call_target="tpu_custom_call" | custom-call | tf_op jit(solution)/shard_map/pallas_call | solution.py:472
  30.0 0.6 %copy.5 = f32[2,32,128]{2,1,0:T(8,128)} copy(f32[2,32,128]{2,1,0:T(8,128)S(1)} %shard_map.37) | data formatting | bytes 65536

commit v8 on v7

--- a/solution.py
+++ b/solution.py
@@ -89,9 +89,20 @@
     far = [hops(ny_dev, (i + 1) // nd_dev) + hops(nd_dev, (i + 1) % nd_dev) / 2 for i in range(len(near))]
     far += [hops(nz_dev, i + 1) for i in range(len(along))] * 2 + [2] * len(corners)
     greeted = near + along + cross_core + corners
+    unmet = 0
     for i in sorted(range(len(greeted)), key=lambda i: -far[i]):
         peer = greeted[i]
-        pl.semaphore_signal(barrier, inc=1, device_id=peer, device_id_type=MESH)
+        dy, dd = (i + 1) // nd_dev, (i + 1) % nd_dev
+        apart = i < len(near) and dd % 2 == 0 and not (dd == 0 and 2 * dy != ny_dev)
+        unmet += apart
+
+        def greet(peer=peer):
+            pl.semaphore_signal(barrier, inc=1, device_id=peer, device_id_type=MESH)
+
+        if apart:
+            pl.when(core == 1)(greet)
+        else:
+            greet()
     for piece in loads[1:]:
         for copy in piece:
             copy.start()
@@ -171,7 +182,7 @@
     edge[1] = jnp.where(odd, pltpu.roll(rims[1], nz - 1, 1), rims[0])
 
     mark("p02b_barrier")
-    pl.semaphore_wait(barrier, len(near) + len(along) + len(cross_core) + len(corners))
+    pl.semaphore_wait(barrier, len(greeted) - unmet * (1 - core))
     mark("p03_halo")
 
     def remote(src, dst, send, recv, peer):

time: 30.7 us -> 30.7 us (level); the launches traced: 30.6 us -> 30.3 us
  Pallas kernels: 30 us -> 29.6 us
    pallas_call x1, Pallas kernels: 30 us -> 29.6 us  [on_device(): pl.pallas_call(functools.partial(kernel, ny_dev, nz_dev, nd_dev), out_sha...]
where the time goes in v8:
time: 30.7 us; the launch traced here: 30.3 us
  Pallas kernels  29.6 us (96%)
  local copies, waits for them, and re-layouts  0.62 us (2%)
    pallas_call x1, Pallas kernels, on_device(): pl.pallas_call(functools.partial(kernel, ny_dev, nz_dev, nd_dev), out_sha...  29.6 us
    unnamed x1, local copies, waits for them, and re-layouts  0.62 us

profile of v8, /device:TPU:4, one launch (start us, length us, event | category | flops | bytes accessed | tf_op | source)
XLA Modules:
  0.0 30.3 jit_solution(13842816362328722622)
XLA Ops:
  0.0 29.6 %shard_map.37 = f32[2,32,128]{2,1,0:T(8,128)S(1)} custom-call(s32[2,4]{1,0:T(2,128)} %box_hbm.1, f32[2,64,32,128]{3,2,1,0:T(8,128)} %corr.1, f32[2,64,32,128]{3,2,1,0:T(8,128)} %illum.1), custom_call_target="tpu_custom_call" | custom-call | tf_op jit(solution)/shard_map/pallas_call | solution.py:483
  29.7 0.6 %copy.5 = f32[2,32,128]{2,1,0:T(8,128)} copy(f32[2,32,128]{2,1,0:T(8,128)S(1)} %shard_map.37) | data formatting | bytes 65536

commit v9 on v7

--- a/solution.py
+++ b/solution.py
@@ -12,7 +12,7 @@
 NORM_ROWS = 16
 FILTER_ROWS = 16
 PAD = 8
-REACH = (3, -3, 1, -1, 0)
+REACH = (3, -3, 1, 0, -1)
 EARLY = ((0, 3), (0, -3))
 F32 = jnp.float32
 MESH = pl.DeviceIdType.MESH

time: 30.7 us -> 30.7 us (level)
  no operation moved by 1% of the time
where the time goes in v9:
time: 30.7 us; the launch traced here: 30.6 us
  Pallas kernels  30 us (98%)
  local copies, waits for them, and re-layouts  0.62 us (2%)
    pallas_call x1, Pallas kernels, on_device(): pl.pallas_call(functools.partial(kernel, ny_dev, nz_dev, nd_dev), out_sha...  30 us
    unnamed x1, local copies, waits for them, and re-layouts  0.62 us

profile of v9, /device:TPU:4, one launch (start us, length us, event | category | flops | bytes accessed | tf_op | source)
XLA Modules:
  0.0 30.6 jit_solution(2992677728934052918)
XLA Ops:
  0.0 30.0 %shard_map.37 = f32[2,32,128]{2,1,0:T(8,128)S(1)} custom-call(s32[2,4]{1,0:T(2,128)} %box_hbm.1, f32[2,64,32,128]{3,2,1,0:T(8,128)} %corr.1, f32[2,64,32,128]{3,2,1,0:T(8,128)} %illum.1), custom_call_target="tpu_custom_call" | custom-call | tf_op jit(solution)/shard_map/pallas_call | solution.py:472
  30.0 0.6 %copy.5 = f32[2,32,128]{2,1,0:T(8,128)} copy(f32[2,32,128]{2,1,0:T(8,128)S(1)} %shard_map.37) | data formatting | bytes 65536
